TPU v7x, 256 devices: a whole 4x4x8 slice. The times are simulated.
256 devices in a mesh: fft: 32 (over x_lo, z, core), scal: 8 (over x_hi, y).
Axes of the slice: x: 4 (x_hi: 2, x_lo: 2; x = x_hi * 2 + x_lo), y: 4, z: 8, core: 2. Of those that a mesh axis runs over, the one named last changes fastest.
Arguments:
- scalar_state: float32 [8, 2, 256, 256, 128], P('scal', None, 'fft'), may hold values from -12 to 12
- velocity: bfloat16 [3, 256, 256, 256], P(None, 'fft', 'scal'), may hold values from -6 to 6
- species: int32 [8], P('scal'), may hold values from 0 to 63
- kappa_table: float32 [64], replicated, may hold values from 0.1 to 1
- dealias_bound: int32 [8], P('scal'), may hold values from 64 to 85
Outputs:
- new_state: float32 [8, 2, 256, 256, 128], P('scal', None, 'fft')
- kappa: float32 [8], P('scal')
All inputs are finite; a program needn't handle non-finite values.
Results may differ from a plain program's by a relative error of at most 0.0027.
Values may be sent and summed in bfloat16 or wider, within the bound.
A program may use at most 128 MiB of HBM per device.

v0:
```python
import math

import jax
import jax.numpy as jnp
from jax import lax
from jax.sharding import PartitionSpec as P

cfl_number = 0.2


def in_one_piece(arrays, axis, split_dim, concat_dim, along):
    widths = [a.shape[along] for a in arrays]
    both = jnp.concatenate(arrays, axis=along)
    out = lax.all_to_all(both, axis, split_axis=split_dim, concat_axis=concat_dim, tiled=True)
    return tuple(jnp.split(out, [sum(widths[:k]) for k in range(1, len(widths))], axis=along))


def copy_for_each(x, axis):
    count = lax.axis_size(axis)
    return lax.all_to_all(jnp.broadcast_to(x[None], (count, *x.shape)), axis, 0, 0, tiled=True)


def collected_together(x, axis):
    leaves = jax.tree.leaves(x)
    sequence = sorted(range(len(leaves)), key=lambda k: -leaves[k].size)
    width = (1, *leaves[sequence[0]].shape)[-1]
    lines = [
        jnp.pad(leaves[k].reshape(-1), (0, -leaves[k].size % width)).reshape(-1, width)
        for k in sequence
    ]
    both, at, found = (copy_for_each(jnp.concatenate(lines), axis), 0, {})
    for k, line in zip(sequence, lines):
        section = both[:, at : at + len(line)].reshape(len(both), -1)
        found[k] = section[:, : leaves[k].size].reshape(-1, *leaves[k].shape)
        at += len(line)
    numbers = iter(range(len(leaves)))
    return jax.tree.map(lambda _: found[next(numbers)], x)


def folded_in_pairs(pieces, combine):
    while len(jax.tree.leaves(pieces)[0]) > 1:
        pieces = jax.vmap(combine)(
            *(jax.tree.map(lambda part: part[side::2], pieces) for side in (0, 1))
        )
    return jax.tree.map(lambda part: part[0], pieces)


def combined_all(x, axis, combine):
    pieces = collected_together(x, axis)
    return folded_in_pairs(pieces, combine)


def twiddle(size_in, size_out, length):
    row_index = jnp.arange(size_in, dtype=jnp.int32)[:, None]
    col_index = jnp.arange(size_out, dtype=jnp.int32)[None, :]
    angles = (row_index * col_index % length).astype(jnp.float32) * (2.0 * math.pi / length)
    norming = 1.0 / math.sqrt(length)
    return (jnp.cos(angles) * norming, jnp.sin(angles) * norming)


def build_tables(length):
    half_len = length // 2
    full_cos, full_sin = twiddle(length, length, length)
    inv_cos, inv_sin = twiddle(half_len, length, length)
    weight = jnp.where(jnp.arange(half_len, dtype=jnp.int32) == 0, 1.0, 2.0).astype(jnp.float32)[
        :, None
    ]
    fwd_cos, fwd_sin = twiddle(length, half_len, length)
    listed = (full_cos, full_sin, inv_cos * weight, inv_sin * weight, fwd_cos, fwd_sin)
    return tuple((matrix.astype(jnp.bfloat16) for matrix in listed))


def product(formula, operand, matrix):
    return jnp.einsum(formula, operand, matrix, preferred_element_type=jnp.float32)


def complex_section(real_part, imag_part, cos_matrix, sin_matrix, formula, inverse):
    real_cos = product(formula, real_part, cos_matrix)
    real_sin = product(formula, real_part, sin_matrix)
    imag_cos = product(formula, imag_part, cos_matrix)
    imag_sin = product(formula, imag_part, sin_matrix)
    if inverse:
        return (real_cos - imag_sin, real_sin + imag_cos)
    return (real_cos + imag_sin, imag_cos - real_sin)


def combine_stats(earlier, later):
    return (earlier[0] + later[0], earlier[1] + later[1], jnp.maximum(earlier[2], later[2]))


def times_wave(wavenumber, real_part, imag_part):
    new_real = (-wavenumber * imag_part.astype(jnp.float32)).astype(jnp.bfloat16)
    new_imag = (wavenumber * real_part.astype(jnp.float32)).astype(jnp.bfloat16)
    return (new_real, new_imag)


def body(scalar_state, velocity, species, kappa_table, dealias_bound):
    ky_local = scalar_state.shape[2]
    length = scalar_state.shape[3]
    half_len = length // 2
    total_count = kappa_table.shape[0]
    full_cos, full_sin, inv_cos, inv_sin, fwd_cos, fwd_sin = build_tables(length)
    ky_index = lax.axis_index("fft") * ky_local + jnp.arange(ky_local, dtype=jnp.int32)
    ky_wave = jnp.where(ky_index < half_len, ky_index, ky_index - length).astype(jnp.float32)[
        :, None, None
    ]
    kz_index = jnp.arange(length, dtype=jnp.int32)
    signed_full = jnp.where(kz_index < half_len, kz_index, kz_index - length).astype(jnp.float32)
    kz_wave = signed_full[None, :, None]
    ky_whole = signed_full[:, None, None]
    kx_wave = jnp.arange(half_len, dtype=jnp.int32).astype(jnp.float32)[None, None, :]
    ksquare = kx_wave * kx_wave + ky_wave * ky_wave + kz_wave * kz_wave
    weight = jnp.where(kx_wave == 0.0, 1.0, 2.0).astype(jnp.float32)
    cell_count = float(length) ** 3
    step_size = cfl_number * 2.0 * math.pi / length
    speeds = lax.all_gather(velocity, "scal", axis=2, tiled=True)

    def finish_inverse(halves):
        y_section = complex_section(
            halves[0], halves[1], full_cos, full_sin, "...yzx,yw->...zwx", True
        )
        y_real = y_section[0].astype(jnp.bfloat16)
        y_imag = y_section[1].astype(jnp.bfloat16)
        return product("...zwk,kx->...zwx", y_real, inv_cos) - product(
            "...zwk,kx->...zwx", y_imag, inv_sin
        )

    def gradient_set(real_part, imag_part):
        pair_real = jnp.stack([real_part, -kz_wave * imag_part]).astype(jnp.bfloat16)
        pair_imag = jnp.stack([imag_part, kz_wave * real_part]).astype(jnp.bfloat16)
        z_section = complex_section(
            pair_real, pair_imag, full_cos, full_sin, "...ykx,kz->...yzx", True
        )
        z_real = z_section[0].astype(jnp.bfloat16)
        z_imag = z_section[1].astype(jnp.bfloat16)
        came_real, came_imag = in_one_piece((z_real, z_imag), "fft", 2, 1, 0)
        x_real, x_imag = times_wave(kx_wave, came_real[0], came_imag[0])
        y_real, y_imag = times_wave(ky_whole, came_real[0], came_imag[0])
        all_real = jnp.stack([x_real, y_real, came_real[1]])
        all_imag = jnp.stack([x_imag, y_imag, came_imag[1]])
        return finish_inverse((all_real, all_imag))

    def advect(gradients):
        total = speeds[0].astype(jnp.float32) * gradients[0]
        total = total + speeds[1].astype(jnp.float32) * gradients[1]
        total = total + speeds[2].astype(jnp.float32) * gradients[2]
        return total.astype(jnp.bfloat16)

    def finish_forward(halves):
        return complex_section(halves[0], halves[1], full_cos, full_sin, "...wzk,zv->...wvk", False)

    def tendency(advected, bound):
        real_x = product("zyx,xk->zyk", advected, fwd_cos).astype(jnp.bfloat16)
        imag_x = (-product("zyx,xk->zyk", advected, fwd_sin)).astype(jnp.bfloat16)
        y_section = complex_section(real_x, imag_x, full_cos, full_sin, "zyk,yw->wzk", False)
        y_real = y_section[0].astype(jnp.bfloat16)
        y_imag = y_section[1].astype(jnp.bfloat16)
        spectral = finish_forward(
            (
                lax.all_to_all(y_real, "fft", split_axis=0, concat_axis=1, tiled=True),
                lax.all_to_all(y_imag, "fft", split_axis=0, concat_axis=1, tiled=True),
            )
        )
        dealias_mask = (ksquare <= bound * bound).astype(jnp.float32)
        return (-dealias_mask * spectral[0], -dealias_mask * spectral[1])

    scalar = 0
    start_real = scalar_state[scalar, 0]
    start_imag = scalar_state[scalar, 1]
    energy = start_real * start_real + start_imag * start_imag
    local_var = [jnp.sum(weight * energy) / cell_count]
    local_grad = [jnp.sum(weight * ksquare * energy) / cell_count]
    gradients = gradient_set(start_real, start_imag)
    magnitude = jnp.sqrt(
        gradients[0] * gradients[0] + gradients[1] * gradients[1] + gradients[2] * gradients[2]
    )
    local_peak = [jnp.max(magnitude)]
    advect_saved = [advect(gradients)]
    var_part = jnp.stack(local_var)
    grad_part = jnp.stack(local_grad)
    peak_part = jnp.stack(local_peak)
    variance, mean_grad, peak_value = combined_all(
        (var_part, grad_part, peak_part), "fft", combine_stats
    )
    matches = species[:, None] == jnp.arange(total_count, dtype=jnp.int32)[None, :]
    base_kappa = jnp.sum(jnp.where(matches, kappa_table[None, :], 0.0), axis=1)
    kappa = base_kappa * peak_value * jnp.sqrt(variance) / (mean_grad + 1e-06)
    scalar = 0
    start_real = scalar_state[scalar, 0]
    start_imag = scalar_state[scalar, 1]
    factor = jnp.exp(-kappa[scalar] * ksquare * step_size)
    bound = dealias_bound[scalar].astype(jnp.float32)
    first_real, first_imag = tendency(advect_saved[scalar], bound)
    mid_real = factor * (start_real + step_size * first_real)
    mid_imag = factor * (start_imag + step_size * first_imag)
    second_real, second_imag = tendency(advect(gradient_set(mid_real, mid_imag)), bound)
    new_real = factor * start_real + 0.5 * step_size * (factor * first_real + second_real)
    new_imag = factor * start_imag + 0.5 * step_size * (factor * first_imag + second_imag)
    updated_list = [jnp.stack([new_real, new_imag])]
    return (jnp.stack(updated_list), kappa)


def solution(mesh):
    placed = (
        P("scal", None, "fft", None, None),
        P(None, "fft", "scal", None),
        P("scal"),
        P(),
        P("scal"),
    )
    return jax.shard_map(
        body,
        mesh=mesh,
        in_specs=placed,
        out_specs=(P("scal", None, "fft", None, None), P("scal")),
        check_vma=False,
    )
```

profile of v0, /device:TPU:1, one launch (start us, length us, event | category | flops | bytes accessed | tf_op | source)
XLA Modules:
  0.0 341.0 jit_solution(12632958124329488233)
XLA Ops:
  7.2 1.9 bitcast_convert_fusion
  9.7 1.4 fusion.55
  11.1 1.3 fusion.56
  12.4 1.4 fusion.13
  13.8 1.4 fusion.12
  15.3 2.7 copy.71
  18.0 11.1 %all-to-all-start = ((bf16[4,8,256,128]{3,1,0,2:T(8,128)(2,1)}), bf16[4,8,256,128]{3,1,0,2:T(8,128)(2,1)}, u32[]{:S(2)}, u32[]{:S(2)}) async-start(bf16[4,8,256,128]{3,1,0,2:T(8,128)(2,1)} %copy.71), calls=%async_computation | async-start | bytes 4194304 | tf_op jit(solution)/shard_map/all_to_all | solution.py:14
  29.9 0.9 multiply_reduce_fusion
  32.1 46.3 %all-to-all-done = bf16[4,8,256,128]{3,1,0,2:T(8,128)(2,1)} async-done(((bf16[4,8,256,128]{3,1,0,2:T(8,128)(2,1)}), bf16[4,8,256,128]{3,1,0,2:T(8,128)(2,1)}, u32[]{:S(2)}, u32[]{:S(2)}) %all-to-all-start) | async-done | bytes 2097184 | tf_op jit(solution)/shard_map/all_to_all | solution.py:14
  78.4 2.4 copy.150
  82.1 3.1 fusion.60
  85.2 3.1 fusion.59
  88.3 1.1 multiply_convert_fusion.7
  89.4 7.1 %fusion.10 = f32[3,8,256,256]{3,2,1,0:T(8,128)} fusion(f32[256,3,8,128]{3,0,2,1:T(8,128)} %fusion.60, bf16[1,256,8,128]{3,1,2,0:T(8,128)(2,1)S(1)} %copy.82, bf16[1,256,8,128]{3,1,2,0:T(8,128)(2,1)} %get-tuple-element.32, bf16[1,256,8,128]{3,1,2,0:T(8,128)(2,1)S(1)} %get-tuple-element.31, f32[128]{0:T(128)S(1)} %fusion.155), kind=kOutput, calls=%fused_computation.39 | convolution fusion | flops 813170688 | bytes 11010560 | tf_op jit(solution)/shard_map/...zwk,kx->...zwx/dot_general | solution.py:74
  96.5 9.0 %convolution_subtract_fusion.1 = f32[3,8,256,256]{3,2,1,0:T(8,128)} fusion(f32[3,8,256,256]{3,2,1,0:T(8,128)} %fusion.10, f32[256,3,8,128]{3,0,2,1:T(8,128)} %fusion.59, bf16[1,256,8,128]{3,1,2,0:T(8,128)(2,1)S(1)} %copy.82, bf16[1,256,8,128]{3,1,2,0:T(8,128)(2,1)} %get-tuple-element.32, bf16[1,256,8,128]{3,1,2,0:T(8,128)(2,1)S(1)} %get-tuple-element.31, ...), kind=kOutput, calls=%fused_computation.5 | convolution fusion | flops 814743552 | bytes 17302016 | tf_op jit(solution)/shard_map/...zwk,kx->...zwx/dot_general | solution.py:74
  105.5 5.7 %sqrt_reduce_fusion = (f32[]{:T(128)}, bf16[8,256,256]{2,1,0:T(8,128)(2,1)S(1)}) fusion(f32[3,8,256,256]{3,2,1,0:T(8,128)} %convolution_subtract_fusion.1, bf16[3,8,256,256]{3,2,1,0:T(8,128)(2,1)} %all-gather.2.cloned.1.call-done), kind=kLoop, calls=%fused_computation.23 | loop fusion | flops 7864319 | bytes 10485764 | tf_op jit(solution)/shard_map/reduce_max | solution.py:177
  111.3 1.4 fusion.32
  112.7 1.7 convolution_convert_fusion.1
  114.4 1.2 fusion.110
  116.9 6.6 %all-to-all-start.1 = ((f32[32,3,1]{1,2,0:T(1,128)}), f32[32,3,1]{1,2,0:T(1,128)S(1)}, u32[]{:S(2)}, u32[]{:S(2)}) async-start(f32[32,3,1]{1,2,0:T(1,128)} %broadcast_in_dim.23), calls=%async_computation.1 | async-start | bytes 32768 | tf_op jit(solution)/shard_map/all_to_all | solution.py:20
  123.5 2.2 fusion.35
  125.8 1.1 copy.85
  126.9 4.5 %all-to-all-done.1 = f32[32,3,1]{1,2,0:T(1,128)S(1)} async-done(((f32[32,3,1]{1,2,0:T(1,128)}), f32[32,3,1]{1,2,0:T(1,128)S(1)}, u32[]{:S(2)}, u32[]{:S(2)}) %all-to-all-start.1) | async-done | bytes 416 | tf_op jit(solution)/shard_map/all_to_all | solution.py:20
  131.4 4.3 %all-to-all-start.3 = ((bf16[256,8,128]{2,1,0:T(8,128)(2,1)}), bf16[256,8,128]{2,1,0:T(8,128)(2,1)S(1)}, u32[]{:S(2)}, u32[]{:S(2)}) async-start(bf16[256,8,128]{2,1,0:T(8,128)(2,1)} %copy.85), calls=%async_computation.3 | async-start | bytes 1048576 | tf_op jit(solution)/shard_map/all_to_all | solution.py:161
  135.8 2.2 fusion.113
  138.0 1.2 fusion.34
  139.2 1.1 copy.83
  140.4 12.1 %all-to-all-done.3 = bf16[256,8,128]{2,1,0:T(8,128)(2,1)S(1)} async-done(((bf16[256,8,128]{2,1,0:T(8,128)(2,1)}), bf16[256,8,128]{2,1,0:T(8,128)(2,1)S(1)}, u32[]{:S(2)}, u32[]{:S(2)}) %all-to-all-start.3) | async-done | bytes 524320 | tf_op jit(solution)/shard_map/all_to_all | solution.py:161
  152.5 5.8 %all-to-all-start.2 = ((bf16[256,8,128]{2,1,0:T(8,128)(2,1)}), bf16[256,8,128]{2,1,0:T(8,128)(2,1)S(1)}, u32[]{:S(2)}, u32[]{:S(2)}) async-start(bf16[256,8,128]{2,1,0:T(8,128)(2,1)} %copy.83), calls=%async_computation.2 | async-start | bytes 1048576 | tf_op jit(solution)/shard_map/all_to_all | solution.py:160
  160.2 0.9 slice_reduce_fusion
  169.8 2.2 fusion.72
  172.0 2.8 all-to-all-done.2
  174.8 1.2 fusion.70
  176.0 2.5 fusion.29
  178.5 1.2 fusion.31
  180.7 1.3 fusion.53
  182.0 1.3 fusion.54
  183.4 1.4 fusion.15
  184.8 1.4 fusion.14
  186.5 1.4 copy.87
  187.9 54.4 %all_to_all.107 = bf16[4,8,256,128]{3,1,0,2:T(8,128)(2,1)S(1)} all-to-all(bf16[4,8,256,128]{3,1,0,2:T(8,128)(2,1)S(1)} %copy.87), channel_id=1, replica_groups=mesh['fft'=32,'scal'=8] {'fft'}, dimensions={2} | all-to-all | bytes 4194304 | tf_op jit(solution)/shard_map/all_to_all | solution.py:14
  244.0 3.1 fusion.58
  247.1 3.1 fusion.57
  250.6 1.1 multiply_convert_fusion.1
  251.7 7.1 %fusion.7 = f32[3,8,256,256]{3,2,1,0:T(8,128)} fusion(f32[256,3,8,128]{3,0,2,1:T(8,128)} %fusion.58, bf16[1,256,8,128]{3,1,2,0:T(8,128)(2,1)S(1)} %copy.98, bf16[1,256,8,128]{3,1,2,0:T(8,128)(2,1)} %get-tuple-element.28, bf16[1,256,8,128]{3,1,2,0:T(8,128)(2,1)S(1)} %get-tuple-element.27, f32[128]{0:T(128)S(1)} %fusion.155), kind=kOutput, calls=%fused_computation.36 | convolution fusion | flops 813170688 | bytes 11010560 | tf_op jit(solution)/shard_map/...zwk,kx->...zwx/dot_general | solution.py:74
  258.8 8.9 %convolution_subtract_fusion = f32[3,8,256,256]{3,2,1,0:T(8,128)} fusion(f32[3,8,256,256]{3,2,1,0:T(8,128)} %fusion.7, f32[256,3,8,128]{3,0,2,1:T(8,128)} %fusion.57, bf16[1,256,8,128]{3,1,2,0:T(8,128)(2,1)S(1)} %copy.98, bf16[1,256,8,128]{3,1,2,0:T(8,128)(2,1)} %get-tuple-element.28, bf16[1,256,8,128]{3,1,2,0:T(8,128)(2,1)S(1)} %get-tuple-element.27, ...), kind=kOutput, calls=%fused_computation.4 | convolution fusion | flops 814743552 | bytes 17302016 | tf_op jit(solution)/shard_map/...zwk,kx->...zwx/dot_general | solution.py:74
  267.7 4.5 %fusion.48 = bf16[8,256,256]{2,1,0:T(8,128)(2,1)S(1)} fusion(f32[3,8,256,256]{3,2,1,0:T(8,128)} %convolution_subtract_fusion, bf16[3,8,256,256]{3,2,1,0:T(8,128)(2,1)} %all-gather.2.cloned.1.call-done), kind=kLoop, calls=%fused_computation.89 | loop fusion | flops 4718592 | bytes 10485760 | tf_op jit(solution)/shard_map/add | solution.py:146
  272.2 0.9 fusion.33
  273.1 1.3 convolution_convert_fusion
  274.4 1.2 fusion.104
  275.6 1.2 fusion.37
  276.9 1.1 copy.101
  278.0 5.9 %all-to-all-start.6 = ((bf16[256,8,128]{2,1,0:T(8,128)(2,1)}), bf16[256,8,128]{2,1,0:T(8,128)(2,1)S(1)}, u32[]{:S(2)}, u32[]{:S(2)}) async-start(bf16[256,8,128]{2,1,0:T(8,128)(2,1)} %copy.101), calls=%async_computation.6 | async-start | bytes 1048576 | tf_op jit(solution)/shard_map/all_to_all | solution.py:161
  283.9 2.2 fusion.107
  286.1 1.2 fusion.36
  287.4 1.2 copy.99
  288.5 12.0 %all-to-all-done.6 = bf16[256,8,128]{2,1,0:T(8,128)(2,1)S(1)} async-done(((bf16[256,8,128]{2,1,0:T(8,128)(2,1)}), bf16[256,8,128]{2,1,0:T(8,128)(2,1)S(1)}, u32[]{:S(2)}, u32[]{:S(2)}) %all-to-all-start.6) | async-done | bytes 524320 | tf_op jit(solution)/shard_map/all_to_all | solution.py:161
  301.3 6.6 %all-to-all-start.5 = ((bf16[256,8,128]{2,1,0:T(8,128)(2,1)}), bf16[256,8,128]{2,1,0:T(8,128)(2,1)}, u32[]{:S(2)}, u32[]{:S(2)}) async-start(bf16[256,8,128]{2,1,0:T(8,128)(2,1)} %copy.99), calls=%async_computation.5 | async-start | bytes 1048576 | tf_op jit(solution)/shard_map/all_to_all | solution.py:160
  307.9 3.3 fusion.66
  311.2 13.2 %all-to-all-done.5 = bf16[256,8,128]{2,1,0:T(8,128)(2,1)} async-done(((bf16[256,8,128]{2,1,0:T(8,128)(2,1)}), bf16[256,8,128]{2,1,0:T(8,128)(2,1)}, u32[]{:S(2)}, u32[]{:S(2)}) %all-to-all-start.5) | async-done | bytes 524320 | tf_op jit(solution)/shard_map/all_to_all | solution.py:160
  324.5 2.2 fusion.64
  326.7 3.0 fusion.21
  329.8 1.5 fusion.27
  331.4 1.5 maximum_bitcast_fusion
  (98 shorter events, 13.2 us)
Async XLA Ops:
  7.2 2.2 copy-start
  18.0 60.4 %all-to-all-start = ((bf16[4,8,256,128]{3,1,0,2:T(8,128)(2,1)}), bf16[4,8,256,128]{3,1,0,2:T(8,128)(2,1)}, u32[]{:S(2)}, u32[]{:S(2)}) async-start(bf16[4,8,256,128]{3,1,0,2:T(8,128)(2,1)} %copy.71), calls=%async_computation | async-start | bytes 4194304 | tf_op jit(solution)/shard_map/all_to_all | solution.py:14
  29.1 76.4 %all-gather.2.cloned.1.call-start = ((), (), s32[]{:S(2)}) async-start(), calls=%async_computation.7 | async-start | bytes 3538944 | tf_op jit(solution)/shard_map/all_gather | solution.py:116
  112.7 1.7 copy-start.7
  116.9 14.5 %all-to-all-start.1 = ((f32[32,3,1]{1,2,0:T(1,128)}), f32[32,3,1]{1,2,0:T(1,128)S(1)}, u32[]{:S(2)}, u32[]{:S(2)}) async-start(f32[32,3,1]{1,2,0:T(1,128)} %broadcast_in_dim.23), calls=%async_computation.1 | async-start | bytes 32768 | tf_op jit(solution)/shard_map/all_to_all | solution.py:20
  125.8 12.2 %copy-start.8 = (bf16[8,256,128]{2,1,0:T(8,128)(2,1)S(1)}, bf16[8,256,128]{2,1,0:T(8,128)(2,1)}, u32[]{:S(2)}) copy-start(bf16[8,256,128]{2,1,0:T(8,128)(2,1)} %copy-done.7) | copy-start | bytes 1572868
  131.4 21.0 %all-to-all-start.3 = ((bf16[256,8,128]{2,1,0:T(8,128)(2,1)}), bf16[256,8,128]{2,1,0:T(8,128)(2,1)S(1)}, u32[]{:S(2)}, u32[]{:S(2)}) async-start(bf16[256,8,128]{2,1,0:T(8,128)(2,1)} %copy.85), calls=%async_computation.3 | async-start | bytes 1048576 | tf_op jit(solution)/shard_map/all_to_all | solution.py:161
  138.0 21.5 %copy-start.10 = (f32[64]{0:T(128)S(1)}, f32[64]{0:T(128)}, u32[]{:S(2)}) copy-start(f32[64]{0:T(128)} %param.8) | copy-start | bytes 772
  152.5 22.3 %all-to-all-start.2 = ((bf16[256,8,128]{2,1,0:T(8,128)(2,1)}), bf16[256,8,128]{2,1,0:T(8,128)(2,1)S(1)}, u32[]{:S(2)}, u32[]{:S(2)}) async-start(bf16[256,8,128]{2,1,0:T(8,128)(2,1)} %copy.83), calls=%async_computation.2 | async-start | bytes 1048576 | tf_op jit(solution)/shard_map/all_to_all | solution.py:160
  178.5 2.1 copy-start.3
  179.7 1.0 copy-start.1
  274.4 2.4 copy-start.9
  278.0 22.5 %all-to-all-start.6 = ((bf16[256,8,128]{2,1,0:T(8,128)(2,1)}), bf16[256,8,128]{2,1,0:T(8,128)(2,1)S(1)}, u32[]{:S(2)}, u32[]{:S(2)}) async-start(bf16[256,8,128]{2,1,0:T(8,128)(2,1)} %copy.101), calls=%async_computation.6 | async-start | bytes 1048576 | tf_op jit(solution)/shard_map/all_to_all | solution.py:161
  300.5 0.8 copy-start.5
  301.3 23.2 %all-to-all-start.5 = ((bf16[256,8,128]{2,1,0:T(8,128)(2,1)}), bf16[256,8,128]{2,1,0:T(8,128)(2,1)}, u32[]{:S(2)}, u32[]{:S(2)}) async-start(bf16[256,8,128]{2,1,0:T(8,128)(2,1)} %copy.99), calls=%async_computation.5 | async-start | bytes 1048576 | tf_op jit(solution)/shard_map/all_to_all | solution.py:160
  307.9 18.8 %copy-start.4 = (f32[8,256,128]{2,1,0:T(8,128)S(1)}, f32[8,256,128]{2,1,0:T(8,128)}, u32[]{:S(2)}) copy-start(f32[8,256,128]{2,1,0:T(8,128)} %copy-done.3) | copy-start | bytes 3145732
  326.7 3.1 copy-start.2
  326.7 3.1 copy-start.6
Sparse Core Ops, SparseCore 0:
  32.5 72.3 all-gather.1
where the time goes:
time: 348 us; the launch traced here: 341 us
  waiting for transfers between devices  91.2 us (26%)
  matrix products  90.6 us (26%)
  blocking collectives  54.4 us (16%)
  starting transfers between devices  40.6 us (12%)
  between operations  23 us (7%)
  local copies, waits for them, and re-layouts  21.8 us (6%)
  other arithmetic  19.3 us (6%)
    dot_general x36, matrix products, product(): jnp.einsum(formula, operand, matrix, preferred_element_type=jnp.float32)  90.6 us
    all_to_all x1, blocking collectives, in_one_piece(): lax.all_to_all(both, axis, split_axis=split_dim, concat_axis=concat_dim,...  54.4 us
    all_to_all x1, waiting for transfers between devices, in_one_piece(): lax.all_to_all(both, axis, split_axis=split_dim, concat_axis=concat_dim,...  46.3 us
    all_to_all x2, waiting for transfers between devices, tendency(): lax.all_to_all(y_imag, 'fft', split_axis=0, concat_axis=1, tiled=True)  24.1 us
    all_to_all x2, waiting for transfers between devices, tendency(): lax.all_to_all(y_real, 'fft', split_axis=0, concat_axis=1, tiled=True)  16 us
    all_to_all x2, starting transfers between devices, tendency(): lax.all_to_all(y_real, 'fft', split_axis=0, concat_axis=1, tiled=True)  12.4 us
    all_to_all x1, starting transfers between devices, in_one_piece(): lax.all_to_all(both, axis, split_axis=split_dim, concat_axis=concat_dim,...  11.1 us
    all_to_all x2, starting transfers between devices, tendency(): lax.all_to_all(y_imag, 'fft', split_axis=0, concat_axis=1, tiled=True)  10.2 us
  transfers between devices with their start and end apart: 7, of which 6 were waited for; matrix products, arithmetic and copies ran while one was open for 15% of the time, Pallas kernels for 0%

commit v1 on v0

v1 whole, which is shorter than its diff:
```python
import functools
import math

import jax
import jax.numpy as jnp
import numpy as np
from jax import lax
from jax.experimental import pallas as pl
from jax.experimental.pallas import tpu as pltpu
from jax.sharding import PartitionSpec as P

MESH = pl.DeviceIdType.MESH
cfl_number = 0.2
LARGEST_BOUND = 85
F32, BF16 = jnp.float32, jnp.bfloat16


def base_tables(length):
    index = np.arange(length)
    angles = (index[:, None] * index[None, :] % length).astype(np.float32) * np.float32(2.0 * math.pi / length)
    norming = np.float32(1.0 / math.sqrt(length))
    cos = (np.cos(angles).astype(np.float32) * norming).astype(np.float32)
    sin = (np.sin(angles).astype(np.float32) * norming).astype(np.float32)
    return cos, sin


def kept_slabs(length, parts):
    rows = length // parts
    signed = np.where(np.arange(length) < length // 2, np.arange(length), np.arange(length) - length)
    return [d for d in range(parts) if np.min(np.abs(signed[d * rows : (d + 1) * rows])) <= LARGEST_BOUND]


def build_tables(length, parts):
    cos, sin = base_tables(length)
    half, rows = length // 2, length // parts
    weight = np.where(np.arange(half) == 0, 1.0, 2.0).astype(np.float32)[:, None]
    real = np.stack([cos, -sin], axis=1)
    imag = np.stack([sin, cos], axis=1)
    inverse = np.stack([real, imag]).transpose(0, 3, 2, 1)
    turned = np.stack([np.stack([-sin, -cos], 1), np.stack([cos, -sin], 1)]).transpose(0, 3, 2, 1)
    forward = np.stack([np.stack([cos, sin], 1), np.stack([-sin, cos], 1)]).transpose(0, 3, 2, 1)
    size = 2 * length

    def slab_columns(table):
        return table.reshape(size, 2, parts, rows).transpose(0, 2, 1, 3).reshape(size, size)

    def slab_rows(table):
        return table.transpose(1, 0, 2, 3).reshape(size, size)

    kept = kept_slabs(length, parts)
    z_inv = slab_rows(inverse)
    y_inv = slab_columns(inverse)
    y_inv_turned = slab_columns(turned)
    y_fwd = slab_rows(forward).reshape(parts, 2 * rows, size)[kept].reshape(-1, size)
    z_fwd = slab_columns(forward)
    x_inv = np.concatenate([cos[:half] * weight, -(sin[:half] * weight)], axis=0)
    x_fwd = np.concatenate([cos[:, :half], -sin[:, :half]], axis=1)
    listed = (z_inv, y_inv, y_inv_turned, y_fwd, z_fwd, x_inv, x_fwd)
    return tuple(jnp.asarray(t.astype(np.float32)).astype(BF16) for t in listed)


def dot(a, b):
    return jnp.dot(a, b, preferred_element_type=F32)


def signed_of(index, length):
    return jnp.where(index < length // 2, index, index - length).astype(F32)


def kernel(
    parts, groups, near,
    state, velocity, species, table, bound,
    z_inv, y_inv, y_inv_turned, y_fwd, z_fwd, x_inv, x_fwd,
    out, kappa_out,
    spec, work, sent, came, speeds, grads, lines, flat, back_sent, back_came, stats,
    send_sem, came_sem, back_send_sem, back_sem, stat_send_sem, stat_sem, vel_sem, vel_send, vel_recv,
):
    rows, length, half = state.shape[1], state.shape[2], state.shape[3]
    kept = kept_slabs(length, parts)
    low = sum(1 for d in kept if d < parts // 2)
    gap = parts - len(kept)
    planes = length // parts
    pairs = planes // 2
    step_size = cfl_number * 2.0 * math.pi / length
    cell_count = float(length) ** 3
    me = lax.axis_index("fft")
    mine = lax.axis_index("scal")
    far = lax.rem(mine + groups // 2, groups)
    upper = (mine // near) * near
    up = upper + lax.rem(mine + 1, near)
    down = upper + lax.rem(mine + near - 1, near)
    far_up, far_down = lax.rem(up + groups // 2, groups), lax.rem(down + groups // 2, groups)
    across = upper + lax.rem(mine + 2, near)
    far_across = lax.rem(across + groups // 2, groups)

    barrier = pltpu.get_barrier_semaphore()

    @pl.loop(1, parts)
    def _(k):
        pl.semaphore_signal(barrier, inc=1, device_id={"fft": lax.rem(me + k, parts)}, device_id_type=MESH)

    for peer in (far, up, down):
        pl.semaphore_signal(barrier, inc=1, device_id={"scal": peer}, device_id_type=MESH)

    own_speeds = pltpu.make_async_copy(velocity, speeds.at[mine], vel_sem)
    own_speeds.start()

    kz = signed_of(lax.broadcasted_iota(jnp.int32, (length, 1), 0), length)
    kx_index = lax.broadcasted_iota(jnp.int32, (1, half), 1)
    kx = kx_index.astype(F32)
    weight = jnp.where(kx_index == 0, 1.0, 2.0).astype(F32)

    def square(row):
        ky = signed_of(me * rows + row, length)
        return kx * kx + ky * ky + kz * kz

    def put_spectrum(row, real, imag):
        spec[row, :length, :half] = real.astype(BF16)
        spec[row, length:, :half] = imag.astype(BF16)
        spec[row, :length, half:] = (-kz * imag).astype(BF16)
        spec[row, length:, half:] = (kz * real).astype(BF16)

    def fold(x):
        return jnp.sum(x.reshape(length // 8, 8, half), axis=0)

    def first_row(row, total):
        real, imag = state[0, row], state[1, row]
        put_spectrum(row, real, imag)
        energy = weight * (real * real + imag * imag)
        return total[0] + fold(energy), total[1] + fold(square(row) * energy)

    zero = jnp.zeros((8, half), F32)
    variance_part, grad_part = lax.fori_loop(0, rows, first_row, (zero, zero))

    batch = 8
    batch_rows = batch * 2 * planes

    def came_copy(turn, chunk, peer):
        return pltpu.make_async_remote_copy(
            src_ref=sent.at[peer, pl.ds(2 * chunk, 2)],
            dst_ref=came.at[pl.ds(2 * chunk, 2), me],
            send_sem=send_sem.at[turn],
            recv_sem=came_sem.at[turn * pairs + chunk],
            device_id={"fft": peer},
            device_id_type=MESH,
        )

    def send_planes(turn):
        def one_batch(k, _):
            which = lax.rem(me // batch + k, parts // batch)
            at = pl.multiple_of(which * batch_rows, batch_rows)

            @pl.loop(0, rows)
            def _(row):
                work[row] = dot(z_inv[pl.ds(at, batch_rows), :], spec[row])

            @pl.loop(0, batch)
            def _(j):
                peer = which * batch + j
                start = pl.multiple_of(j * 2 * planes, 2 * planes)
                block = work[:, pl.ds(start, 2 * planes), :]
                turned = jnp.swapaxes(block, 0, 1).reshape(planes, 2 * rows, 2 * half).astype(BF16)
                sent[peer] = turned

                @pl.when(peer == me)
                def _():
                    came[:, pl.ds(me, 1)] = turned[:, None]

            if turn == 0:
                @pl.when(k == 0)
                def _():
                    pl.semaphore_wait(barrier, parts - 1 + 3)

            @pl.loop(0, batch)
            def _(j):
                peer = which * batch + j

                @pl.when(peer != me)
                def _():
                    came_copy(turn, 0, peer).start()

            return 0

        lax.fori_loop(0, parts // batch, one_batch, 0)

        @pl.loop(1, pairs)
        def _(chunk):
            @pl.loop(1, parts)
            def _(k):
                came_copy(turn, chunk, lax.rem(me + k, parts)).start()

    def wait_planes(turn, chunk):
        piece = sent.at[pl.ds(0, parts - 1), pl.ds(0, 2)]
        pltpu.make_async_remote_copy(
            src_ref=piece, dst_ref=piece, send_sem=send_sem.at[turn],
            recv_sem=came_sem.at[turn * pairs + chunk], device_id={"fft": me}, device_id_type=MESH,
        ).wait_recv()

    def wait_sent(turn):
        piece = sent.at[pl.ds(0, parts - 1)]
        pltpu.make_async_remote_copy(
            src_ref=piece, dst_ref=piece, send_sem=send_sem.at[turn],
            recv_sem=came_sem.at[turn * pairs], device_id={"fft": me}, device_id_type=MESH,
        ).wait_send()

    ky_row = lax.broadcasted_iota(jnp.int32, (2 * length, 1), 0)
    ky_row = signed_of((ky_row // (2 * rows)) * rows + lax.rem(ky_row, rows), length).astype(BF16)
    kx_low = kx.astype(BF16)

    def to_grid(field, plane, real, imag):
        halves = jnp.concatenate([real, imag], axis=1).astype(BF16)
        grads[field, plane] = dot(halves, x_inv[...])

    def gradient_pair(chunk):
        last = []
        for side in (0, 1):
            plane = 2 * chunk + side
            both = came[plane].reshape(2 * length, 2 * half)
            whole, deriv = both[:, :half], both[:, half:]
            last.append(deriv)
            scaled = jnp.concatenate([whole * kx_low, whole * ky_row], axis=1)
            done = dot(y_inv_turned[...], scaled)
            to_grid(0, plane, done[:length, :half], done[length:, :half])
            to_grid(1, plane, done[:length, half:], done[length:, half:])
        done = dot(y_inv[...], jnp.concatenate(last, axis=1))
        to_grid(2, 2 * chunk, done[:length, :half], done[length:, :half])
        to_grid(2, 2 * chunk + 1, done[:length, half:], done[length:, half:])

    def peak_of(plane, peak):
        gx, gy, gz = grads[0, plane], grads[1, plane], grads[2, plane]
        size = gx * gx + gy * gy + gz * gz
        return jnp.maximum(peak, jnp.max(size.reshape(-1, 8, length), axis=0))

    def forward_pair(chunk):
        for side in (0, 1):
            plane = 2 * chunk + side
            total = speeds[:, 0, plane].reshape(length, length).astype(F32) * grads[0, plane]
            total = total + speeds[:, 1, plane].reshape(length, length).astype(F32) * grads[1, plane]
            total = total + speeds[:, 2, plane].reshape(length, length).astype(F32) * grads[2, plane]
            part = dot(total.astype(BF16), x_fwd[...]).astype(BF16)
            lines[:length, side * half : (side + 1) * half] = part[:, :half]
            lines[length:, side * half : (side + 1) * half] = part[:, half:]
        done = dot(y_fwd[...], lines[...])
        flat[2 * chunk] = done[:, :half]
        flat[2 * chunk + 1] = done[:, half:]

    def back_copy(turn, slot, peer):
        return pltpu.make_async_remote_copy(
            src_ref=back_sent.at[slot], dst_ref=back_came.at[me],
            send_sem=back_send_sem.at[turn], recv_sem=back_sem.at[turn],
            device_id={"fft": peer}, device_id_type=MESH,
        )

    keeps = jnp.logical_or(me < low, me >= low + gap)

    def send_rows(turn):
        @pl.loop(0, len(kept))
        def _(slot):
            peer = jnp.where(slot < low, slot, slot + gap)
            start = pl.multiple_of(slot * 2 * rows, 2 * rows)
            block = flat[:, pl.ds(start, 2 * rows), :]
            turned = jnp.swapaxes(block, 0, 1).reshape(rows, 2 * planes, half).astype(BF16)
            back_sent[slot] = turned

            @pl.when(peer == me)
            def _():
                back_came[pl.ds(me, 1)] = turned[None]

            @pl.when(peer != me)
            def _():
                back_copy(turn, slot, peer).start()

    def wait_rows_sent(turn):
        @pl.when(keeps)
        def _():
            piece = back_sent.at[pl.ds(0, len(kept) - 1)]
            pltpu.make_async_remote_copy(
                src_ref=piece, dst_ref=piece, send_sem=back_send_sem.at[turn],
                recv_sem=back_sem.at[turn], device_id={"fft": me}, device_id_type=MESH,
            ).wait_send()

        @pl.when(jnp.logical_not(keeps))
        def _():
            piece = back_sent.at[pl.ds(0, len(kept))]
            pltpu.make_async_remote_copy(
                src_ref=piece, dst_ref=piece, send_sem=back_send_sem.at[turn],
                recv_sem=back_sem.at[turn], device_id={"fft": me}, device_id_type=MESH,
            ).wait_send()

    def wait_rows(turn):
        @pl.when(keeps)
        def _():
            piece = back_came.at[pl.ds(0, parts - 1)]
            pltpu.make_async_remote_copy(
                src_ref=piece, dst_ref=piece, send_sem=back_send_sem.at[turn],
                recv_sem=back_sem.at[turn], device_id={"fft": me}, device_id_type=MESH,
            ).wait_recv()

    def tendency_pair(pair):
        held = [back_came[:, 2 * pair + side].reshape(2 * length, half) for side in (0, 1)]
        return dot(z_fwd[...], jnp.concatenate(held, axis=1))

    def speeds_copy(k, block, peer, at=None):
        ref = speeds.at[block] if at is None else speeds.at[block, :, pl.ds(at, planes // 2)]
        return pltpu.make_async_remote_copy(
            src_ref=ref, dst_ref=ref, send_sem=vel_send.at[k], recv_sem=vel_recv.at[k],
            device_id={"scal": peer}, device_id_type=MESH,
        )

    @pl.when(jnp.logical_not(keeps))
    def _():
        back_came[...] = jnp.zeros_like(back_came)

    own_speeds.wait()
    send_planes(0)
    first = speeds_copy(0, mine, far)
    first.start()
    first.wait_send()
    speeds_copy(0, far, far).wait_recv()
    for k, peer in ((1, up), (3, down)):
        speeds_copy(k, mine, peer).start()
        speeds_copy(k + 1, far, peer).start()

    def half_one(chunk, peak):
        wait_planes(0, chunk)
        gradient_pair(chunk)
        return peak_of(2 * chunk + 1, peak_of(2 * chunk, peak))

    peak = jnp.zeros((8, length), F32)
    peak = lax.fori_loop(0, pairs // 2, half_one, peak)
    cut = planes // 2
    speeds_copy(1, down, up).wait_recv()
    speeds_copy(2, far_down, up).wait_recv()
    speeds_copy(5, down, up, 0).start()
    speeds_copy(6, far_down, up, 0).start()
    speeds_copy(3, up, down).wait_recv()
    speeds_copy(4, far_up, down).wait_recv()
    speeds_copy(7, up, down, cut).start()
    speeds_copy(8, far_up, down, cut).start()
    peak = lax.fori_loop(pairs // 2, pairs, half_one, peak)
    for k, peer in ((1, up), (3, down)):
        speeds_copy(k, mine, peer).wait_send()
        speeds_copy(k + 1, far, peer).wait_send()
    speeds_copy(5, across, up, 0).wait()
    speeds_copy(6, far_across, up, 0).wait()
    speeds_copy(7, across, down, cut).wait()
    speeds_copy(8, far_across, down, cut).wait()

    peak = jnp.maximum(peak[:, :half], peak[:, half:])
    stats[me] = jnp.concatenate(
        [
            jnp.sum(variance_part, axis=0, keepdims=True),
            jnp.sum(grad_part, axis=0, keepdims=True),
            jnp.max(peak, axis=0, keepdims=True),
            jnp.zeros((5, half), F32),
        ],
        axis=0,
    )

    @pl.loop(0, pairs)
    def _(chunk):
        forward_pair(chunk)

    @pl.loop(1, parts)
    def _(k):
        pltpu.make_async_remote_copy(
            src_ref=stats.at[me], dst_ref=stats.at[me], send_sem=stat_send_sem, recv_sem=stat_sem,
            device_id={"fft": lax.rem(me + k, parts)}, device_id_type=MESH,
        ).start()

    send_rows(0)
    wait_sent(0)
    everyone = stats.at[pl.ds(0, parts - 1)]
    stat_wait = pltpu.make_async_remote_copy(
        src_ref=everyone, dst_ref=everyone, send_sem=stat_send_sem, recv_sem=stat_sem,
        device_id={"fft": me}, device_id_type=MESH,
    )
    stat_wait.wait_send()
    stat_wait.wait_recv()
    collected = stats[...]
    variance = jnp.sum(jnp.sum(collected[:, 0], axis=0, keepdims=True), axis=1, keepdims=True) / cell_count
    mean_grad = jnp.sum(jnp.sum(collected[:, 1], axis=0, keepdims=True), axis=1, keepdims=True) / cell_count
    largest = jnp.max(jnp.max(collected[:, 2], axis=0, keepdims=True), axis=1, keepdims=True)
    count = table.shape[1]
    match = lax.broadcasted_iota(jnp.int32, (1, count), 1) == species[0]
    base = jnp.sum(jnp.where(match, table[...], 0.0), axis=1, keepdims=True)
    kappa = base * jnp.sqrt(largest) * jnp.sqrt(variance) / (mean_grad + 1e-06)
    kappa_out[...] = jnp.broadcast_to(kappa, kappa_out.shape)
    limit = bound[0].astype(F32)
    limit = limit * limit

    wait_rows(0)

    @pl.loop(0, rows // 2)
    def _(pair):
        done = tendency_pair(pair)
        for side in (0, 1):
            row = 2 * pair + side
            here = slice(side * half, (side + 1) * half)
            ksquare = square(row)
            keep = ksquare <= limit
            factor = jnp.exp(-kappa * ksquare * step_size)
            moved = []
            for part in (0, 1):
                start = state[part, row]
                rate = jnp.where(keep, -done[part * length : (part + 1) * length, here], 0.0)
                moved.append(factor * (start + step_size * rate))
                out[part, row] = factor * start + 0.5 * step_size * (factor * rate)
            put_spectrum(row, *moved)

    send_planes(1)

    @pl.loop(0, pairs)
    def _(chunk):
        wait_planes(1, chunk)
        gradient_pair(chunk)
        forward_pair(chunk)

    wait_rows_sent(0)
    send_rows(1)
    wait_sent(1)
    wait_rows(1)

    @pl.loop(0, rows // 2)
    def _(pair):
        done = tendency_pair(pair)
        for side in (0, 1):
            row = 2 * pair + side
            here = slice(side * half, (side + 1) * half)
            keep = square(row) <= limit
            for part in (0, 1):
                rate = jnp.where(keep, -done[part * length : (part + 1) * length, here], 0.0)
                out[part, row] = out[part, row] + 0.5 * step_size * rate

    wait_rows_sent(1)


def body(parts, groups, scalar_state, velocity, species, kappa_table, dealias_bound):
    _, _, rows, length, half = scalar_state.shape
    planes = length // parts
    kept = kept_slabs(length, parts)
    tables = build_tables(length, parts)
    near = groups // 2
    chunk_rows = velocity.shape[2]
    vmem = pl.BlockSpec(memory_space=pltpu.VMEM)
    smem = pl.BlockSpec(memory_space=pltpu.SMEM)
    hbm = pl.BlockSpec(memory_space=pl.ANY)
    DMA = pltpu.SemaphoreType.DMA
    new_state, kappa = pl.pallas_call(
        functools.partial(kernel, parts, groups, near),
        out_shape=(
            jax.ShapeDtypeStruct((2, rows, length, half), F32),
            jax.ShapeDtypeStruct((8, half), F32),
        ),
        in_specs=[vmem, hbm, smem, vmem, smem] + [vmem] * len(tables),
        out_specs=(vmem, vmem),
        scratch_shapes=[
            pltpu.VMEM((rows, 2 * length, 2 * half), BF16),
            pltpu.VMEM((rows, 16 * planes, 2 * half), F32),
            pltpu.VMEM((parts, planes, 2 * rows, 2 * half), BF16),
            pltpu.VMEM((planes, parts, 2 * rows, 2 * half), BF16),
            pltpu.VMEM((groups, 3, planes, chunk_rows, length), BF16),
            pltpu.VMEM((3, planes, length, length), F32),
            pltpu.VMEM((2 * length, 2 * half), BF16),
            pltpu.VMEM((planes, len(kept) * 2 * rows, half), F32),
            pltpu.VMEM((len(kept), rows, 2 * planes, half), BF16),
            pltpu.VMEM((parts, rows, 2 * planes, half), BF16),
            pltpu.VMEM((parts, 8, half), F32),
            DMA((2,)),
            DMA((planes,)),
            DMA((2,)),
            DMA((2,)),
            DMA,
            DMA,
            DMA,
            DMA((9,)),
            DMA((9,)),
        ],
        compiler_params=pltpu.CompilerParams(
            collective_id=0, has_side_effects=True, vmem_limit_bytes=60 * 1024 * 1024
        ),
    )(scalar_state[0], velocity, species, kappa_table[None, :], dealias_bound, *tables)
    return new_state[None], kappa[0, :1]


def solution(mesh):
    parts, groups = mesh.shape["fft"], mesh.shape["scal"]
    placed = (
        P("scal", None, "fft", None, None),
        P(None, "fft", "scal", None),
        P("scal"),
        P(),
        P("scal"),
    )
    return jax.shard_map(
        functools.partial(body, parts, groups),
        mesh=mesh,
        in_specs=placed,
        out_specs=(P("scal", None, "fft", None, None), P("scal")),
        check_vma=False,
    )
```

time: 348 us -> 182 us (0.52); the launches traced: 341 us -> 180 us
  Pallas kernels: 0 us -> 174 us
  waiting for transfers between devices: 91.2 us -> 0 us
  matrix products: 90.6 us -> 0 us
  blocking collectives: 54.4 us -> 0 us
  starting transfers between devices: 40.6 us -> 0 us
  between operations: 23 us -> 1.93 us
  other arithmetic: 19.3 us -> 0 us
  local copies, waits for them, and re-layouts: 21.8 us -> 4.3 us
    pallas_call x0 -> x1, Pallas kernels: none -> 174 us  [body(): pl.pallas_call(functools.partial(kernel, parts, groups, near), out_shape=...]
    all_to_all x6 -> x0, waiting for transfers between devices: 90.8 us -> none  [the longest x1 46.3 us: in_one_piece(): lax.all_to_all(both, axis, split_axis=split_dim, concat_axis=concat_dim,...]
    dot_general x36 -> x0, matrix products: 90.6 us -> none  [product(): jnp.einsum(formula, operand, matrix, preferred_element_type=jnp.float32)]
    all_to_all x1 -> x0, blocking collectives: 54.4 us -> none  [in_one_piece(): lax.all_to_all(both, axis, split_axis=split_dim, concat_axis=concat_dim,...]
    all_to_all x6 -> x0, starting transfers between devices: 40.3 us -> none  [the longest x2 12.4 us: tendency(): lax.all_to_all(y_real, 'fft', split_axis=0, concat_axis=1, tiled=True)]
    reduce_max x1 -> x0, other arithmetic: 5.75 us -> none  [body(): local_peak = [jnp.max(magnitude)]]
    convert_element_type x8 -> x0, local copies, waits for them, and re-layouts: 5.03 us -> none  [the longest x2 2.29 us: tendency(): y_real = y_section[0].astype(jnp.bfloat16)]
    slice x36 -> x1, local copies, waits for them, and re-layouts: 5.84 us -> 1.19 us  [body(): return (new_state[None], kappa[0, :1])]
  transfers between devices with their start and end apart: 7 -> 0, of which waited for: 6 -> 0; matrix products, arithmetic and copies ran while one was open for 15% -> 0% of each run, Pallas kernels for 0% -> 0%
where the time goes in v1:
time: 182 us; the launch traced here: 180 us
  Pallas kernels  174 us (96%)
  local copies, waits for them, and re-layouts  4.3 us (2%)
  between operations  1.93 us (1%)
    pallas_call x1, Pallas kernels, body(): pl.pallas_call(functools.partial(kernel, parts, groups, near), out_shape=...  174 us

profile of v1, /device:TPU:1, one launch (start us, length us, event | category | flops | bytes accessed | tf_op | source)
XLA Modules:
  0.0 179.9 jit_solution(13265482217980347446)
XLA Ops:
  1.9 173.6 %shard_map.131 = (f32[2,8,256,128]{3,2,1,0:T(8,128)}, f32[8,128]{1,0:T(8,128)}) custom-call(f32[2,8,256,128]{3,2,1,0:T(8,128)} %bitcast.4, bf16[3,8,32,256]{3,2,1,0:T(8,128)(2,1)} %velocity.1, s32[1]{0:T(128)S(6)} %copy.15.species, f32[1,64]{1,0:T(1,128)} %bitcast.6, s32[1]{0:T(128)S(6)} %copy.16.bound, bf16[512,512]{1,0:T(8,128)(2,1)} %constant.25.z_inv, ...), custom_call_target="tpu_custom_call" | custom-call | tf_op jit(solution)/shard_map/pallas_call | solution.py:449
  175.6 1.2 slice.3
  176.8 3.1 %copy.17 = f32[1,2,8,256,128]{4,3,2,1,0:T(8,128)} copy(f32[1,2,8,256,128]{4,3,2,1,0:T(8,128)} %bitcast.5) | data formatting | bytes 4194304

commit v2 on v1

--- a/solution.py
+++ b/solution.py
@@ -28,6 +28,18 @@
     rows = length // parts
     signed = np.where(np.arange(length) < length // 2, np.arange(length), np.arange(length) - length)
     return [d for d in range(parts) if np.min(np.abs(signed[d * rows : (d + 1) * rows])) <= LARGEST_BOUND]
+
+
+def narrow_slots(length, parts, half):
+    rows = length // parts
+    thin = []
+    for slot, d in enumerate(kept_slabs(length, parts)):
+        ky = np.arange(d * rows, (d + 1) * rows)
+        least = np.min(np.abs(np.where(ky < length // 2, ky, ky - length)))
+        if LARGEST_BOUND**2 - least**2 < (half // 2) ** 2:
+            thin.append(slot)
+    assert thin == list(range(thin[0], thin[-1] + 1))
+    return thin[0], thin[-1] + 1
 
 
 def build_tables(length, parts):
@@ -170,6 +182,7 @@
                 @pl.when(k == 0)
                 def _():
                     pl.semaphore_wait(barrier, parts - 1 + 3)
+                    speeds_copy(0, mine, far).start()
 
             @pl.loop(0, batch)
             def _(j):
@@ -244,61 +257,115 @@
         flat[2 * chunk] = done[:, :half]
         flat[2 * chunk + 1] = done[:, half:]
 
-    def back_copy(turn, slot, peer):
+    quads = rows // 4
+    keeps = jnp.logical_or(me < low, me >= low + gap)
+    my_slot = jnp.where(me < low, me, me - gap)
+    thin_low, thin_high = narrow_slots(length, parts, half)
+    my_thin = jnp.logical_and(keeps, jnp.logical_and(my_slot >= thin_low, my_slot < thin_high))
+    my_wide = jnp.logical_and(keeps, jnp.logical_not(my_thin))
+    lane = lax.broadcasted_iota(jnp.int32, (1, half), 1)
+
+    def back_copy(turn, quad, slot, peer, tiles):
         return pltpu.make_async_remote_copy(
-            src_ref=back_sent.at[slot], dst_ref=back_came.at[me],
-            send_sem=back_send_sem.at[turn], recv_sem=back_sem.at[turn],
+            src_ref=back_sent.at[quad, slot, pl.ds(0, tiles)], dst_ref=back_came.at[quad, me, pl.ds(0, tiles)],
+            send_sem=back_send_sem.at[turn], recv_sem=back_sem.at[quads * turn + quad],
             device_id={"fft": peer}, device_id_type=MESH,
         )
 
-    keeps = jnp.logical_or(me < low, me >= low + gap)
+    def turn_lanes(x, amount):
+        return pltpu.roll(x, amount, x.ndim - 1)
+
+    def packed(block):
+        a, b, c, d = (block[k] for k in range(4))
+        left = lane < half // 2
+        ends = jnp.where(
+            left,
+            jnp.where(lane < half // 4, turn_lanes(a, half // 2), turn_lanes(b, 3 * half // 4)),
+            jnp.where(lane < 3 * half // 4, c, turn_lanes(d, half // 4)),
+        )
+        return jnp.stack(
+            [
+                jnp.where(left, a, turn_lanes(b, half // 2)),
+                jnp.where(left, c, turn_lanes(d, half // 2)),
+                ends,
+            ]
+        )
+
+    def unpacked(quad):
+        first, second, ends = (
+            back_came[quad, :, k].reshape(2 * length, half) for k in range(3)
+        )
+        left = lane < half // 2
+        return (
+            jnp.where(left, first, turn_lanes(ends, half // 2)),
+            jnp.where(left, turn_lanes(first, half // 2), turn_lanes(ends, half // 4)),
+            jnp.where(left, second, ends),
+            jnp.where(left, turn_lanes(second, half // 2), turn_lanes(ends, 3 * half // 4)),
+        )
 
     def send_rows(turn):
-        @pl.loop(0, len(kept))
-        def _(slot):
+        def one(at, _):
+            quad, slot = at // len(kept), lax.rem(at, len(kept))
             peer = jnp.where(slot < low, slot, slot + gap)
-            start = pl.multiple_of(slot * 2 * rows, 2 * rows)
-            block = flat[:, pl.ds(start, 2 * rows), :]
-            turned = jnp.swapaxes(block, 0, 1).reshape(rows, 2 * planes, half).astype(BF16)
-            back_sent[slot] = turned
+            start = pl.multiple_of(slot * 2 * rows + quad * 8, 8)
+            block = jnp.swapaxes(flat[:, pl.ds(start, 8), :], 0, 1).reshape(4, 2 * planes, half)
+            tiles = packed(block).astype(BF16)
+            back_sent[quad, slot] = tiles
 
             @pl.when(peer == me)
             def _():
-                back_came[pl.ds(me, 1)] = turned[None]
-
-            @pl.when(peer != me)
+                back_came[quad, me] = tiles
+
+            thin = jnp.logical_and(slot >= thin_low, slot < thin_high)
+
+            @pl.when(jnp.logical_and(peer != me, thin))
             def _():
-                back_copy(turn, slot, peer).start()
+                back_copy(turn, quad, slot, peer, 2).start()
+
+            @pl.when(jnp.logical_and(peer != me, jnp.logical_not(thin)))
+            def _():
+                back_copy(turn, quad, slot, peer, 3).start()
+
+            return 0
+
+        lax.fori_loop(0, quads * len(kept), one, 0)
 
     def wait_rows_sent(turn):
-        @pl.when(keeps)
-        def _():
-            piece = back_sent.at[pl.ds(0, len(kept) - 1)]
-            pltpu.make_async_remote_copy(
-                src_ref=piece, dst_ref=piece, send_sem=back_send_sem.at[turn],
-                recv_sem=back_sem.at[turn], device_id={"fft": me}, device_id_type=MESH,
-            ).wait_send()
-
-        @pl.when(jnp.logical_not(keeps))
-        def _():
-            piece = back_sent.at[pl.ds(0, len(kept))]
-            pltpu.make_async_remote_copy(
-                src_ref=piece, dst_ref=piece, send_sem=back_send_sem.at[turn],
-                recv_sem=back_sem.at[turn], device_id={"fft": me}, device_id_type=MESH,
-            ).wait_send()
-
-    def wait_rows(turn):
-        @pl.when(keeps)
-        def _():
-            piece = back_came.at[pl.ds(0, parts - 1)]
-            pltpu.make_async_remote_copy(
-                src_ref=piece, dst_ref=piece, send_sem=back_send_sem.at[turn],
-                recv_sem=back_sem.at[turn], device_id={"fft": me}, device_id_type=MESH,
-            ).wait_recv()
-
-    def tendency_pair(pair):
-        held = [back_came[:, 2 * pair + side].reshape(2 * length, half) for side in (0, 1)]
-        return dot(z_fwd[...], jnp.concatenate(held, axis=1))
+        thin_count = thin_high - thin_low
+        wide_count = len(kept) - thin_count
+        for quad in range(quads):
+            for tiles, count, own in ((2, thin_count, my_thin), (3, wide_count, my_wide)):
+                @pl.when(own)
+                def _():
+                    sent_tiles(turn, tiles, count - 1).wait_send()
+
+                @pl.when(jnp.logical_not(own))
+                def _():
+                    sent_tiles(turn, tiles, count).wait_send()
+
+    def sent_tiles(turn, tiles, count):
+        piece = back_sent.at[0, pl.ds(0, count), pl.ds(0, tiles)]
+        return pltpu.make_async_remote_copy(
+            src_ref=piece, dst_ref=piece, send_sem=back_send_sem.at[turn],
+            recv_sem=back_sem.at[quads * turn], device_id={"fft": me}, device_id_type=MESH,
+        )
+
+    def wait_rows(turn, quad):
+        for tiles, own in ((2, my_thin), (3, my_wide)):
+            @pl.when(own)
+            def _():
+                piece = back_came.at[0, pl.ds(0, parts - 1), pl.ds(0, tiles)]
+                pltpu.make_async_remote_copy(
+                    src_ref=piece, dst_ref=piece, send_sem=back_send_sem.at[turn],
+                    recv_sem=back_sem.at[quads * turn + quad], device_id={"fft": me}, device_id_type=MESH,
+                ).wait_recv()
+
+    def tendency(quad, use):
+        held = unpacked(quad)
+        for pair in (0, 1):
+            done = dot(z_fwd[...], jnp.concatenate(held[2 * pair : 2 * pair + 2], axis=1))
+            for side in (0, 1):
+                use(4 * quad + 2 * pair + side, done[:, side * half : (side + 1) * half])
 
     def speeds_copy(k, block, peer, at=None):
         ref = speeds.at[block] if at is None else speeds.at[block, :, pl.ds(at, planes // 2)]
@@ -307,15 +374,13 @@
             device_id={"scal": peer}, device_id_type=MESH,
         )
 
-    @pl.when(jnp.logical_not(keeps))
+    @pl.when(jnp.logical_not(my_wide))
     def _():
         back_came[...] = jnp.zeros_like(back_came)
 
     own_speeds.wait()
     send_planes(0)
-    first = speeds_copy(0, mine, far)
-    first.start()
-    first.wait_send()
+    speeds_copy(0, mine, far).wait_send()
     speeds_copy(0, far, far).wait_recv()
     for k, peer in ((1, up), (3, down)):
         speeds_copy(k, mine, peer).start()
@@ -337,14 +402,28 @@
     speeds_copy(4, far_up, down).wait_recv()
     speeds_copy(7, up, down, cut).start()
     speeds_copy(8, far_up, down, cut).start()
-    peak = lax.fori_loop(pairs // 2, pairs, half_one, peak)
-    for k, peer in ((1, up), (3, down)):
-        speeds_copy(k, mine, peer).wait_send()
-        speeds_copy(k + 1, far, peer).wait_send()
-    speeds_copy(5, across, up, 0).wait()
-    speeds_copy(6, far_across, up, 0).wait()
-    speeds_copy(7, across, down, cut).wait()
-    speeds_copy(8, far_across, down, cut).wait()
+
+    def half_two(chunk, peak):
+        peak = half_one(chunk, peak)
+        late = chunk == pairs - 2
+
+        @pl.when(late)
+        def _():
+            for k, peer in ((1, up), (3, down)):
+                speeds_copy(k, mine, peer).wait_send()
+                speeds_copy(k + 1, far, peer).wait_send()
+            speeds_copy(5, across, up, 0).wait()
+            speeds_copy(6, far_across, up, 0).wait()
+            speeds_copy(7, across, down, cut).wait()
+            speeds_copy(8, far_across, down, cut).wait()
+
+        @pl.loop(jnp.where(late, 0, chunk), chunk + 1)
+        def _(k):
+            forward_pair(k)
+
+        return peak
+
+    peak = lax.fori_loop(pairs // 2, pairs, half_two, peak)
 
     peak = jnp.maximum(peak[:, :half], peak[:, half:])
     stats[me] = jnp.concatenate(
@@ -356,10 +435,6 @@
         ],
         axis=0,
     )
-
-    @pl.loop(0, pairs)
-    def _(chunk):
-        forward_pair(chunk)
 
     @pl.loop(1, parts)
     def _(k):
@@ -389,24 +464,22 @@
     limit = bound[0].astype(F32)
     limit = limit * limit
 
-    wait_rows(0)
-
-    @pl.loop(0, rows // 2)
-    def _(pair):
-        done = tendency_pair(pair)
-        for side in (0, 1):
-            row = 2 * pair + side
-            here = slice(side * half, (side + 1) * half)
-            ksquare = square(row)
-            keep = ksquare <= limit
-            factor = jnp.exp(-kappa * ksquare * step_size)
-            moved = []
-            for part in (0, 1):
-                start = state[part, row]
-                rate = jnp.where(keep, -done[part * length : (part + 1) * length, here], 0.0)
-                moved.append(factor * (start + step_size * rate))
-                out[part, row] = factor * start + 0.5 * step_size * (factor * rate)
-            put_spectrum(row, *moved)
+    def to_middle(row, done):
+        ksquare = square(row)
+        keep = ksquare <= limit
+        factor = jnp.exp(-kappa * ksquare * step_size)
+        moved = []
+        for part in (0, 1):
+            start = state[part, row]
+            rate = jnp.where(keep, -done[part * length : (part + 1) * length], 0.0)
+            moved.append(factor * (start + step_size * rate))
+            out[part, row] = factor * start + 0.5 * step_size * (factor * rate)
+        put_spectrum(row, *moved)
+
+    @pl.loop(0, quads)
+    def _(quad):
+        wait_rows(0, quad)
+        tendency(quad, to_middle)
 
     send_planes(1)
 
@@ -419,18 +492,17 @@
     wait_rows_sent(0)
     send_rows(1)
     wait_sent(1)
-    wait_rows(1)
-
-    @pl.loop(0, rows // 2)
-    def _(pair):
-        done = tendency_pair(pair)
-        for side in (0, 1):
-            row = 2 * pair + side
-            here = slice(side * half, (side + 1) * half)
-            keep = square(row) <= limit
-            for part in (0, 1):
-                rate = jnp.where(keep, -done[part * length : (part + 1) * length, here], 0.0)
-                out[part, row] = out[part, row] + 0.5 * step_size * rate
+
+    def to_end(row, done):
+        keep = square(row) <= limit
+        for part in (0, 1):
+            rate = jnp.where(keep, -done[part * length : (part + 1) * length], 0.0)
+            out[part, row] = out[part, row] + 0.5 * step_size * rate
+
+    @pl.loop(0, quads)
+    def _(quad):
+        wait_rows(1, quad)
+        tendency(quad, to_end)
 
     wait_rows_sent(1)
 
@@ -463,13 +535,13 @@
             pltpu.VMEM((3, planes, length, length), F32),
             pltpu.VMEM((2 * length, 2 * half), BF16),
             pltpu.VMEM((planes, len(kept) * 2 * rows, half), F32),
-            pltpu.VMEM((len(kept), rows, 2 * planes, half), BF16),
-            pltpu.VMEM((parts, rows, 2 * planes, half), BF16),
+            pltpu.VMEM((rows // 4, len(kept), 3, 2 * planes, half), BF16),
+            pltpu.VMEM((rows // 4, parts, 3, 2 * planes, half), BF16),
             pltpu.VMEM((parts, 8, half), F32),
             DMA((2,)),
             DMA((planes,)),
             DMA((2,)),
-            DMA((2,)),
+            DMA((rows // 2,)),
             DMA,
             DMA,
             DMA,

time: 182 us -> 157 us (0.86)
  Pallas kernels: 174 us -> 149 us
    pallas_call x1, Pallas kernels: 174 us -> 149 us  [body(): pl.pallas_call(functools.partial(kernel, parts, groups, near), out_shape=...]
where the time goes in v2:
time: 157 us; the launch traced here: 155 us
  Pallas kernels  149 us (95%)
  local copies, waits for them, and re-layouts  4.3 us (3%)
  between operations  1.93 us (1%)
    pallas_call x1, Pallas kernels, body(): pl.pallas_call(functools.partial(kernel, parts, groups, near), out_shape=...  149 us

profile of v2, /device:TPU:1, one launch (start us, length us, event | category | flops | bytes accessed | tf_op | source)
XLA Modules:
  0.0 154.8 jit_solution(16837523281059687051)
XLA Ops:
  1.9 148.5 %shard_map.131 = (f32[2,8,256,128]{3,2,1,0:T(8,128)}, f32[8,128]{1,0:T(8,128)}) custom-call(f32[2,8,256,128]{3,2,1,0:T(8,128)} %bitcast.4, bf16[3,8,32,256]{3,2,1,0:T(8,128)(2,1)} %velocity.1, s32[1]{0:T(128)S(6)} %copy.15.species, f32[1,64]{1,0:T(1,128)} %bitcast.6, s32[1]{0:T(128)S(6)} %copy.16.bound, bf16[512,512]{1,0:T(8,128)(2,1)} %constant.25.z_inv, ...), custom_call_target="tpu_custom_call" | custom-call | tf_op jit(solution)/shard_map/pallas_call | solution.py:521
  150.5 1.2 slice.3
  151.6 3.1 %copy.17 = f32[1,2,8,256,128]{4,3,2,1,0:T(8,128)} copy(f32[1,2,8,256,128]{4,3,2,1,0:T(8,128)} %bitcast.5) | data formatting | bytes 4194304

commit v3 on v2

--- a/solution.py
+++ b/solution.py
@@ -42,6 +42,14 @@
     return thin[0], thin[-1] + 1
 
 
+def batch_order(parts):
+    ring = parts // 4
+    return [
+        column * (parts // 2) + (place + side * (ring // 2)) * 2 + core
+        for place in range(ring // 2) for column in (0, 1) for side in (0, 1) for core in (0, 1)
+    ]
+
+
 def build_tables(length, parts):
     cos, sin = base_tables(length)
     half, rows = length // 2, length // parts
@@ -60,7 +68,7 @@
         return table.transpose(1, 0, 2, 3).reshape(size, size)
 
     kept = kept_slabs(length, parts)
-    z_inv = slab_rows(inverse)
+    z_inv = slab_rows(inverse).reshape(parts, 2 * rows, size)[batch_order(parts)].reshape(size, size)
     y_inv = slab_columns(inverse)
     y_inv_turned = slab_columns(turned)
     y_fwd = slab_rows(forward).reshape(parts, 2 * rows, size)[kept].reshape(-1, size)
@@ -82,11 +90,13 @@
 def kernel(
     parts, groups, near,
     state, velocity, species, table, bound,
-    z_inv, y_inv, y_inv_turned, y_fwd, z_fwd, x_inv, x_fwd,
-    out, kappa_out,
-    spec, work, sent, came, speeds, grads, lines, flat, back_sent, back_came, stats,
-    send_sem, came_sem, back_send_sem, back_sem, stat_send_sem, stat_sem, vel_sem, vel_send, vel_recv,
+    z_inv, *rest,
 ):
+    (
+        *far_tables, out, kappa_out,
+        y_inv, y_inv_turned, y_fwd, z_fwd, x_inv, x_fwd, table_sem, spec, work, sent, came, speeds, grads, lines, flat, back_sent, back_came, stats,
+        send_sem, came_sem, back_send_sem, back_sem, stat_send_sem, stat_sem, vel_sem, vel_send, vel_recv,
+    ) = rest
     rows, length, half = state.shape[1], state.shape[2], state.shape[3]
     kept = kept_slabs(length, parts)
     low = sum(1 for d in kept if d < parts // 2)
@@ -116,6 +126,12 @@
 
     own_speeds = pltpu.make_async_copy(velocity, speeds.at[mine], vel_sem)
     own_speeds.start()
+    table_copies = [
+        pltpu.make_async_copy(src, dst, table_sem.at[k])
+        for k, (src, dst) in enumerate(zip(far_tables, (y_inv, y_inv_turned, y_fwd, z_fwd, x_inv, x_fwd)))
+    ]
+    for copy in table_copies:
+        copy.start()
 
     kz = signed_of(lax.broadcasted_iota(jnp.int32, (length, 1), 0), length)
     kx_index = lax.broadcasted_iota(jnp.int32, (1, half), 1)
@@ -127,25 +143,42 @@
         return kx * kx + ky * ky + kz * kz
 
     def put_spectrum(row, real, imag):
-        spec[row, :length, :half] = real.astype(BF16)
-        spec[row, length:, :half] = imag.astype(BF16)
-        spec[row, :length, half:] = (-kz * imag).astype(BF16)
-        spec[row, length:, half:] = (kz * real).astype(BF16)
+        here = pl.ds(pl.multiple_of(row * 2 * half, 2 * half), half)
+        there = pl.ds(pl.multiple_of(row * 2 * half + half, half), half)
+        spec[:length, here] = real.astype(BF16)
+        spec[length:, here] = imag.astype(BF16)
+        spec[:length, there] = (-kz * imag).astype(BF16)
+        spec[length:, there] = (kz * real).astype(BF16)
 
     def fold(x):
         return jnp.sum(x.reshape(length // 8, 8, half), axis=0)
 
-    def first_row(row, total):
+    @pl.loop(0, rows)
+    def _(row):
+        put_spectrum(row, state[0, row], state[1, row])
+
+    def row_energy(row, total):
         real, imag = state[0, row], state[1, row]
-        put_spectrum(row, real, imag)
         energy = weight * (real * real + imag * imag)
         return total[0] + fold(energy), total[1] + fold(square(row) * energy)
 
-    zero = jnp.zeros((8, half), F32)
-    variance_part, grad_part = lax.fori_loop(0, rows, first_row, (zero, zero))
-
     batch = 8
+    batches = parts // batch
     batch_rows = batch * 2 * planes
+    ring = parts // 4
+    my_place = lax.rem(me // 2, ring)
+
+    def slab_at(column, place, core):
+        return column * (parts // 2) + place * 2 + core
+
+    def peer_in_batch(which, j):
+        return slab_at(j // 4, which + lax.rem(j // 2, 2) * (ring // 2), lax.rem(j, 2))
+
+    def peer_in_turn(i):
+        q = i // 4
+        step = jnp.where(lax.rem(q, 2) == 1, (q + 1) // 2, ring - q // 2)
+        column = lax.rem(me // (parts // 2) + lax.rem(i // 2, 2), 2)
+        return slab_at(column, lax.rem(my_place + step, ring), lax.rem(me + i, 2))
 
     def came_copy(turn, chunk, peer):
         return pltpu.make_async_remote_copy(
@@ -159,34 +192,27 @@
 
     def send_planes(turn):
         def one_batch(k, _):
-            which = lax.rem(me // batch + k, parts // batch)
+            which = lax.rem(my_place + batches // 2 + k, batches)
             at = pl.multiple_of(which * batch_rows, batch_rows)
-
-            @pl.loop(0, rows)
-            def _(row):
-                work[row] = dot(z_inv[pl.ds(at, batch_rows), :], spec[row])
-
-            @pl.loop(0, batch)
-            def _(j):
-                peer = which * batch + j
-                start = pl.multiple_of(j * 2 * planes, 2 * planes)
-                block = work[:, pl.ds(start, 2 * planes), :]
+            work[...] = dot(z_inv[pl.ds(at, batch_rows), :], spec[...])
+            for j in range(batch):
+                peer = peer_in_batch(which, j)
+                strip = work[j * 2 * planes : (j + 1) * 2 * planes, :]
+                block = jnp.stack([strip[:, row * 2 * half : (row + 1) * 2 * half] for row in range(rows)])
                 turned = jnp.swapaxes(block, 0, 1).reshape(planes, 2 * rows, 2 * half).astype(BF16)
                 sent[peer] = turned
-
-                @pl.when(peer == me)
-                def _():
-                    came[:, pl.ds(me, 1)] = turned[:, None]
 
             if turn == 0:
                 @pl.when(k == 0)
                 def _():
                     pl.semaphore_wait(barrier, parts - 1 + 3)
                     speeds_copy(0, mine, far).start()
+                    speeds_copy(1, mine, up).start()
+                    speeds_copy(3, mine, down).start()
 
             @pl.loop(0, batch)
             def _(j):
-                peer = which * batch + j
+                peer = peer_in_batch(which, j)
 
                 @pl.when(peer != me)
                 def _():
@@ -195,12 +221,13 @@
             return 0
 
         lax.fori_loop(0, parts // batch, one_batch, 0)
+        came[:, pl.ds(me, 1)] = sent[me][:, None]
 
         @pl.loop(1, pairs)
         def _(chunk):
             @pl.loop(1, parts)
-            def _(k):
-                came_copy(turn, chunk, lax.rem(me + k, parts)).start()
+            def _(i):
+                came_copy(turn, chunk, peer_in_turn(i)).start()
 
     def wait_planes(turn, chunk):
         piece = sent.at[pl.ds(0, parts - 1), pl.ds(0, 2)]
@@ -303,36 +330,35 @@
             jnp.where(left, turn_lanes(second, half // 2), turn_lanes(ends, 3 * half // 4)),
         )
 
+    thin_count = thin_high - thin_low
+    wide_count = len(kept) - thin_count
+
+    def start_rows(turn, quad, tiles, count, slot_of):
+        @pl.loop(0, count)
+        def _(i):
+            away = jnp.where(lax.rem(i, 2) == 1, (i + 1) // 2, count - i // 2)
+            slot = slot_of(lax.rem(me * count // parts + away, count))
+            peer = jnp.where(slot < low, slot, slot + gap)
+
+            @pl.when(peer != me)
+            def _():
+                back_copy(turn, quad, slot, peer, tiles).start()
+
     def send_rows(turn):
-        def one(at, _):
-            quad, slot = at // len(kept), lax.rem(at, len(kept))
-            peer = jnp.where(slot < low, slot, slot + gap)
-            start = pl.multiple_of(slot * 2 * rows + quad * 8, 8)
-            block = jnp.swapaxes(flat[:, pl.ds(start, 8), :], 0, 1).reshape(4, 2 * planes, half)
-            tiles = packed(block).astype(BF16)
-            back_sent[quad, slot] = tiles
-
-            @pl.when(peer == me)
+        @pl.loop(0, quads)
+        def _(quad):
+            for slot in range(len(kept)):
+                start = pl.multiple_of(slot * 2 * rows + quad * 8, 8)
+                block = jnp.swapaxes(flat[:, pl.ds(start, 8), :], 0, 1).reshape(4, 2 * planes, half)
+                back_sent[quad, slot] = packed(block).astype(BF16)
+            start_rows(turn, quad, 3, wide_count, lambda k: jnp.where(k < thin_low, k, k + thin_count))
+            start_rows(turn, quad, 2, thin_count, lambda k: k + thin_low)
+
+            @pl.when(keeps)
             def _():
-                back_came[quad, me] = tiles
-
-            thin = jnp.logical_and(slot >= thin_low, slot < thin_high)
-
-            @pl.when(jnp.logical_and(peer != me, thin))
-            def _():
-                back_copy(turn, quad, slot, peer, 2).start()
-
-            @pl.when(jnp.logical_and(peer != me, jnp.logical_not(thin)))
-            def _():
-                back_copy(turn, quad, slot, peer, 3).start()
-
-            return 0
-
-        lax.fori_loop(0, quads * len(kept), one, 0)
+                back_came[quad, me] = back_sent[quad, my_slot]
 
     def wait_rows_sent(turn):
-        thin_count = thin_high - thin_low
-        wide_count = len(kept) - thin_count
         for quad in range(quads):
             for tiles, count, own in ((2, thin_count, my_thin), (3, wide_count, my_wide)):
                 @pl.when(own)
@@ -380,11 +406,18 @@
 
     own_speeds.wait()
     send_planes(0)
-    speeds_copy(0, mine, far).wait_send()
+    zero = jnp.zeros((8, half), F32)
+    variance_part, grad_part = lax.fori_loop(0, rows, row_energy, (zero, zero))
+    for copy in table_copies:
+        copy.wait()
+    cut = planes // 2
+    speeds_copy(1, down, up).wait_recv()
+    speeds_copy(5, down, up, 0).start()
+    speeds_copy(3, up, down).wait_recv()
+    speeds_copy(7, up, down, cut).start()
     speeds_copy(0, far, far).wait_recv()
-    for k, peer in ((1, up), (3, down)):
-        speeds_copy(k, mine, peer).start()
-        speeds_copy(k + 1, far, peer).start()
+    speeds_copy(2, far, up).start()
+    speeds_copy(4, far, down).start()
 
     def half_one(chunk, peak):
         wait_planes(0, chunk)
@@ -393,14 +426,9 @@
 
     peak = jnp.zeros((8, length), F32)
     peak = lax.fori_loop(0, pairs // 2, half_one, peak)
-    cut = planes // 2
-    speeds_copy(1, down, up).wait_recv()
     speeds_copy(2, far_down, up).wait_recv()
-    speeds_copy(5, down, up, 0).start()
     speeds_copy(6, far_down, up, 0).start()
-    speeds_copy(3, up, down).wait_recv()
     speeds_copy(4, far_up, down).wait_recv()
-    speeds_copy(7, up, down, cut).start()
     speeds_copy(8, far_up, down, cut).start()
 
     def half_two(chunk, peak):
@@ -409,6 +437,7 @@
 
         @pl.when(late)
         def _():
+            speeds_copy(0, mine, far).wait_send()
             for k, peer in ((1, up), (3, down)):
                 speeds_copy(k, mine, peer).wait_send()
                 speeds_copy(k + 1, far, peer).wait_send()
@@ -425,16 +454,14 @@
 
     peak = lax.fori_loop(pairs // 2, pairs, half_two, peak)
 
-    peak = jnp.maximum(peak[:, :half], peak[:, half:])
-    stats[me] = jnp.concatenate(
-        [
-            jnp.sum(variance_part, axis=0, keepdims=True),
-            jnp.sum(grad_part, axis=0, keepdims=True),
-            jnp.max(peak, axis=0, keepdims=True),
-            jnp.zeros((5, half), F32),
-        ],
-        axis=0,
-    )
+    def whole(reduce, x):
+        return reduce(reduce(x, axis=0, keepdims=True), axis=1, keepdims=True)
+
+    stats[pl.ds(me, 1)] = jnp.where(
+        lane == 0,
+        whole(jnp.sum, variance_part),
+        jnp.where(lane == 1, whole(jnp.sum, grad_part), whole(jnp.max, peak)),
+    )[None]
 
     @pl.loop(1, parts)
     def _(k):
@@ -452,10 +479,11 @@
     )
     stat_wait.wait_send()
     stat_wait.wait_recv()
-    collected = stats[...]
-    variance = jnp.sum(jnp.sum(collected[:, 0], axis=0, keepdims=True), axis=1, keepdims=True) / cell_count
-    mean_grad = jnp.sum(jnp.sum(collected[:, 1], axis=0, keepdims=True), axis=1, keepdims=True) / cell_count
-    largest = jnp.max(jnp.max(collected[:, 2], axis=0, keepdims=True), axis=1, keepdims=True)
+    collected = stats[...].reshape(parts, half)
+    sums = jnp.sum(collected, axis=0, keepdims=True)
+    variance = sums[:, :1] / cell_count
+    mean_grad = sums[:, 1:2] / cell_count
+    largest = jnp.max(collected, axis=0, keepdims=True)[:, 2:3]
     count = table.shape[1]
     match = lax.broadcasted_iota(jnp.int32, (1, count), 1) == species[0]
     base = jnp.sum(jnp.where(match, table[...], 0.0), axis=1, keepdims=True)
@@ -503,6 +531,7 @@
     def _(quad):
         wait_rows(1, quad)
         tendency(quad, to_end)
+
 
     wait_rows_sent(1)
 
@@ -520,15 +549,14 @@
     DMA = pltpu.SemaphoreType.DMA
     new_state, kappa = pl.pallas_call(
         functools.partial(kernel, parts, groups, near),
-        out_shape=(
-            jax.ShapeDtypeStruct((2, rows, length, half), F32),
-            jax.ShapeDtypeStruct((8, half), F32),
-        ),
-        in_specs=[vmem, hbm, smem, vmem, smem] + [vmem] * len(tables),
+        out_shape=(pltpu.VMEM((2, rows, length, half), F32), pltpu.VMEM((8, half), F32)),
+        in_specs=[vmem, hbm, smem, vmem, smem, vmem] + [hbm] * (len(tables) - 1),
         out_specs=(vmem, vmem),
         scratch_shapes=[
-            pltpu.VMEM((rows, 2 * length, 2 * half), BF16),
-            pltpu.VMEM((rows, 16 * planes, 2 * half), F32),
+            *(pltpu.VMEM(t.shape, t.dtype) for t in tables[1:]),
+            DMA((len(tables) - 1,)),
+            pltpu.VMEM((2 * length, rows * 2 * half), BF16),
+            pltpu.VMEM((16 * planes, rows * 2 * half), F32),
             pltpu.VMEM((parts, planes, 2 * rows, 2 * half), BF16),
             pltpu.VMEM((planes, parts, 2 * rows, 2 * half), BF16),
             pltpu.VMEM((groups, 3, planes, chunk_rows, length), BF16),
@@ -537,7 +565,7 @@
             pltpu.VMEM((planes, len(kept) * 2 * rows, half), F32),
             pltpu.VMEM((rows // 4, len(kept), 3, 2 * planes, half), BF16),
             pltpu.VMEM((rows // 4, parts, 3, 2 * planes, half), BF16),
-            pltpu.VMEM((parts, 8, half), F32),
+            pltpu.VMEM((parts, 1, half), F32),
             DMA((2,)),
             DMA((planes,)),
             DMA((2,)),

time: 157 us -> 148 us (0.943)
  Pallas kernels: 149 us -> 143 us
  local copies, waits for them, and re-layouts: 4.3 us -> 1.83 us
    pallas_call x1, Pallas kernels: 149 us -> 143 us  [body(): pl.pallas_call(functools.partial(kernel, parts, groups, near), out_shape=...]
    unnamed x1, local copies, waits for them, and re-layouts: 3.11 us -> 1.32 us
where the time goes in v3:
time: 148 us; the launch traced here: 147 us
  Pallas kernels  143 us (97%)
  between operations  1.93 us (1%)
  local copies, waits for them, and re-layouts  1.83 us (1%)
    pallas_call x1, Pallas kernels, body(): pl.pallas_call(functools.partial(kernel, parts, groups, near), out_shape=...  143 us

profile of v3, /device:TPU:1, one launch (start us, length us, event | category | flops | bytes accessed | tf_op | source)
XLA Modules:
  0.0 147.1 jit_solution(15029742592565908810)
XLA Ops:
  1.9 143.3 %shard_map.131 = (f32[2,8,256,128]{3,2,1,0:T(8,128)S(1)}, f32[8,128]{1,0:T(8,128)S(1)}) custom-call(f32[2,8,256,128]{3,2,1,0:T(8,128)} %bitcast.5, bf16[3,8,32,256]{3,2,1,0:T(8,128)(2,1)} %velocity.1, s32[1]{0:T(128)S(6)} %copy.16.species, f32[1,64]{1,0:T(1,128)} %bitcast.6, s32[1]{0:T(128)S(6)} %copy.17.bound, bf16[512,512]{1,0:T(8,128)(2,1)} %constant.25.z_inv, ...), custom_call_target="tpu_custom_call" | custom-call | tf_op jit(solution)/shard_map/pallas_call | solution.py:550
  145.2 0.5 slice.3
  145.7 1.3 copy.15

commit v4 on v3

--- a/solution.py
+++ b/solution.py
@@ -89,15 +89,14 @@
 
 def kernel(
     parts, groups, near,
-    state, velocity, species, table, bound,
-    z_inv, *rest,
+    state_in, velocity, species, table, bound, *rest,
 ):
     (
         *far_tables, out, kappa_out,
-        y_inv, y_inv_turned, y_fwd, z_fwd, x_inv, x_fwd, table_sem, spec, work, sent, came, speeds, grads, lines, flat, back_sent, back_came, stats,
+        state, state_sem, z_inv, y_inv, y_inv_turned, y_fwd, z_fwd, x_inv, x_fwd, table_sem, spec, work, sent, came, speeds, grads, halves, lines, flat, back_sent, back_came, stats,
         send_sem, came_sem, back_send_sem, back_sem, stat_send_sem, stat_sem, vel_sem, vel_send, vel_recv,
     ) = rest
-    rows, length, half = state.shape[1], state.shape[2], state.shape[3]
+    _, rows, length, half = state.shape
     kept = kept_slabs(length, parts)
     low = sum(1 for d in kept if d < parts // 2)
     gap = parts - len(kept)
@@ -115,6 +114,13 @@
     across = upper + lax.rem(mine + 2, near)
     far_across = lax.rem(across + groups // 2, groups)
 
+    table_copies = [
+        pltpu.make_async_copy(src, dst, table_sem.at[k])
+        for k, (src, dst) in enumerate(zip(far_tables, (z_inv, y_inv, y_inv_turned, y_fwd, z_fwd, x_inv, x_fwd)))
+    ]
+    state_copy = pltpu.make_async_copy(state_in, state, state_sem)
+    state_copy.start()
+    table_copies[0].start()
     barrier = pltpu.get_barrier_semaphore()
 
     @pl.loop(1, parts)
@@ -126,11 +132,7 @@
 
     own_speeds = pltpu.make_async_copy(velocity, speeds.at[mine], vel_sem)
     own_speeds.start()
-    table_copies = [
-        pltpu.make_async_copy(src, dst, table_sem.at[k])
-        for k, (src, dst) in enumerate(zip(far_tables, (y_inv, y_inv_turned, y_fwd, z_fwd, x_inv, x_fwd)))
-    ]
-    for copy in table_copies:
+    for copy in table_copies[1:]:
         copy.start()
 
     kz = signed_of(lax.broadcasted_iota(jnp.int32, (length, 1), 0), length)
@@ -153,9 +155,13 @@
     def fold(x):
         return jnp.sum(x.reshape(length // 8, 8, half), axis=0)
 
+    state_copy.wait()
+
     @pl.loop(0, rows)
     def _(row):
         put_spectrum(row, state[0, row], state[1, row])
+
+    table_copies[0].wait()
 
     def row_energy(row, total):
         real, imag = state[0, row], state[1, row]
@@ -192,7 +198,7 @@
 
     def send_planes(turn):
         def one_batch(k, _):
-            which = lax.rem(my_place + batches // 2 + k, batches)
+            which = lax.rem(my_place + k, batches)
             at = pl.multiple_of(which * batch_rows, batch_rows)
             work[...] = dot(z_inv[pl.ds(at, batch_rows), :], spec[...])
             for j in range(batch):
@@ -227,7 +233,7 @@
         def _(chunk):
             @pl.loop(1, parts)
             def _(i):
-                came_copy(turn, chunk, peer_in_turn(i)).start()
+                came_copy(turn, chunk, peer_in_turn(parts - i)).start()
 
     def wait_planes(turn, chunk):
         piece = sent.at[pl.ds(0, parts - 1), pl.ds(0, 2)]
@@ -247,39 +253,48 @@
     ky_row = signed_of((ky_row // (2 * rows)) * rows + lax.rem(ky_row, rows), length).astype(BF16)
     kx_low = kx.astype(BF16)
 
-    def to_grid(field, plane, real, imag):
-        halves = jnp.concatenate([real, imag], axis=1).astype(BF16)
-        grads[field, plane] = dot(halves, x_inv[...])
-
     def gradient_pair(chunk):
-        last = []
+        scaled, last = [], []
+        for side in (0, 1):
+            both = came[2 * chunk + side].reshape(2 * length, 2 * half)
+            whole = both[:, :half]
+            last.append(both[:, half:])
+            scaled += [whole * kx_low, whole * ky_row]
+
+        def put(done, column, at):
+            here = slice(column * half, (column + 1) * half)
+            halves[at * length : (at + 1) * length, :half] = done[:length, here].astype(BF16)
+            halves[at * length : (at + 1) * length, half:] = done[length:, here].astype(BF16)
+
+        done = dot(y_inv_turned[...], jnp.concatenate(scaled, axis=1))
+        for side in (0, 1):
+            for field in (0, 1):
+                put(done, 2 * side + field, 2 * field + side)
+        done = dot(y_inv[...], jnp.concatenate(last, axis=1))
+        for side in (0, 1):
+            put(done, side, 4 + side)
+        grads[chunk] = dot(halves[...], x_inv[...]).reshape(6, length, length)
+
+    def peak_of(chunk, peak):
+        for side in (0, 1):
+            gx, gy, gz = (grads[chunk, 2 * field + side] for field in range(3))
+            size = gx * gx + gy * gy + gz * gz
+            peak = jnp.maximum(peak, jnp.max(size.reshape(-1, 8, length), axis=0))
+        return peak
+
+    def forward_pair(chunk):
+        terms = []
         for side in (0, 1):
             plane = 2 * chunk + side
-            both = came[plane].reshape(2 * length, 2 * half)
-            whole, deriv = both[:, :half], both[:, half:]
-            last.append(deriv)
-            scaled = jnp.concatenate([whole * kx_low, whole * ky_row], axis=1)
-            done = dot(y_inv_turned[...], scaled)
-            to_grid(0, plane, done[:length, :half], done[length:, :half])
-            to_grid(1, plane, done[:length, half:], done[length:, half:])
-        done = dot(y_inv[...], jnp.concatenate(last, axis=1))
-        to_grid(2, 2 * chunk, done[:length, :half], done[length:, :half])
-        to_grid(2, 2 * chunk + 1, done[:length, half:], done[length:, half:])
-
-    def peak_of(plane, peak):
-        gx, gy, gz = grads[0, plane], grads[1, plane], grads[2, plane]
-        size = gx * gx + gy * gy + gz * gz
-        return jnp.maximum(peak, jnp.max(size.reshape(-1, 8, length), axis=0))
-
-    def forward_pair(chunk):
+            total = speeds[:, 0, plane].reshape(length, length).astype(F32) * grads[chunk, side]
+            total = total + speeds[:, 1, plane].reshape(length, length).astype(F32) * grads[chunk, 2 + side]
+            total = total + speeds[:, 2, plane].reshape(length, length).astype(F32) * grads[chunk, 4 + side]
+            terms.append(total.astype(BF16))
+        part = dot(jnp.concatenate(terms, axis=0), x_fwd[...]).astype(BF16)
         for side in (0, 1):
-            plane = 2 * chunk + side
-            total = speeds[:, 0, plane].reshape(length, length).astype(F32) * grads[0, plane]
-            total = total + speeds[:, 1, plane].reshape(length, length).astype(F32) * grads[1, plane]
-            total = total + speeds[:, 2, plane].reshape(length, length).astype(F32) * grads[2, plane]
-            part = dot(total.astype(BF16), x_fwd[...]).astype(BF16)
-            lines[:length, side * half : (side + 1) * half] = part[:, :half]
-            lines[length:, side * half : (side + 1) * half] = part[:, half:]
+            here, lanes = slice(side * length, (side + 1) * length), slice(side * half, (side + 1) * half)
+            lines[:length, lanes] = part[here, :half]
+            lines[length:, lanes] = part[here, half:]
         done = dot(y_fwd[...], lines[...])
         flat[2 * chunk] = done[:, :half]
         flat[2 * chunk + 1] = done[:, half:]
@@ -333,16 +348,21 @@
     thin_count = thin_high - thin_low
     wide_count = len(kept) - thin_count
 
-    def start_rows(turn, quad, tiles, count, slot_of):
-        @pl.loop(0, count)
+    def start_rows(turn, quad):
+        @pl.loop(1, parts)
         def _(i):
-            away = jnp.where(lax.rem(i, 2) == 1, (i + 1) // 2, count - i // 2)
-            slot = slot_of(lax.rem(me * count // parts + away, count))
-            peer = jnp.where(slot < low, slot, slot + gap)
-
-            @pl.when(peer != me)
+            peer = peer_in_turn(parts - i)
+            slot = jnp.where(peer < low, peer, peer - gap)
+            wanted = jnp.logical_or(peer < low, peer >= low + gap)
+            thin = jnp.logical_and(slot >= thin_low, slot < thin_high)
+
+            @pl.when(jnp.logical_and(wanted, thin))
             def _():
-                back_copy(turn, quad, slot, peer, tiles).start()
+                back_copy(turn, quad, slot, peer, 2).start()
+
+            @pl.when(jnp.logical_and(wanted, jnp.logical_not(thin)))
+            def _():
+                back_copy(turn, quad, slot, peer, 3).start()
 
     def send_rows(turn):
         @pl.loop(0, quads)
@@ -351,8 +371,7 @@
                 start = pl.multiple_of(slot * 2 * rows + quad * 8, 8)
                 block = jnp.swapaxes(flat[:, pl.ds(start, 8), :], 0, 1).reshape(4, 2 * planes, half)
                 back_sent[quad, slot] = packed(block).astype(BF16)
-            start_rows(turn, quad, 3, wide_count, lambda k: jnp.where(k < thin_low, k, k + thin_count))
-            start_rows(turn, quad, 2, thin_count, lambda k: k + thin_low)
+            start_rows(turn, quad)
 
             @pl.when(keeps)
             def _():
@@ -408,7 +427,7 @@
     send_planes(0)
     zero = jnp.zeros((8, half), F32)
     variance_part, grad_part = lax.fori_loop(0, rows, row_energy, (zero, zero))
-    for copy in table_copies:
+    for copy in table_copies[1:]:
         copy.wait()
     cut = planes // 2
     speeds_copy(1, down, up).wait_recv()
@@ -422,7 +441,7 @@
     def half_one(chunk, peak):
         wait_planes(0, chunk)
         gradient_pair(chunk)
-        return peak_of(2 * chunk + 1, peak_of(2 * chunk, peak))
+        return peak_of(chunk, peak)
 
     peak = jnp.zeros((8, length), F32)
     peak = lax.fori_loop(0, pairs // 2, half_one, peak)
@@ -550,17 +569,20 @@
     new_state, kappa = pl.pallas_call(
         functools.partial(kernel, parts, groups, near),
         out_shape=(pltpu.VMEM((2, rows, length, half), F32), pltpu.VMEM((8, half), F32)),
-        in_specs=[vmem, hbm, smem, vmem, smem, vmem] + [hbm] * (len(tables) - 1),
+        in_specs=[hbm, hbm, smem, vmem, smem] + [hbm] * len(tables),
         out_specs=(vmem, vmem),
         scratch_shapes=[
-            *(pltpu.VMEM(t.shape, t.dtype) for t in tables[1:]),
-            DMA((len(tables) - 1,)),
+            pltpu.VMEM((2, rows, length, half), F32),
+            DMA,
+            *(pltpu.VMEM(t.shape, t.dtype) for t in tables),
+            DMA((len(tables),)),
             pltpu.VMEM((2 * length, rows * 2 * half), BF16),
             pltpu.VMEM((16 * planes, rows * 2 * half), F32),
             pltpu.VMEM((parts, planes, 2 * rows, 2 * half), BF16),
             pltpu.VMEM((planes, parts, 2 * rows, 2 * half), BF16),
             pltpu.VMEM((groups, 3, planes, chunk_rows, length), BF16),
-            pltpu.VMEM((3, planes, length, length), F32),
+            pltpu.VMEM((planes // 2, 6, length, length), F32),
+            pltpu.VMEM((6 * length, 2 * half), BF16),
             pltpu.VMEM((2 * length, 2 * half), BF16),
             pltpu.VMEM((planes, len(kept) * 2 * rows, half), F32),
             pltpu.VMEM((rows // 4, len(kept), 3, 2 * planes, half), BF16),

time: 148 us -> 143 us (0.966)
  Pallas kernels: 143 us -> 139 us
    pallas_call x1, Pallas kernels: 143 us -> 139 us  [body(): pl.pallas_call(functools.partial(kernel, parts, groups, near), out_shape=...]
where the time goes in v4:
time: 143 us
  Pallas kernels  139 us (97%)
  between operations  1.93 us (1%)
  local copies, waits for them, and re-layouts  1.83 us (1%)
    pallas_call x1, Pallas kernels, body(): pl.pallas_call(functools.partial(kernel, parts, groups, near), out_shape=...  139 us

profile of v4, /device:TPU:1, one launch (start us, length us, event | category | flops | bytes accessed | tf_op | source)
XLA Modules:
  0.0 142.7 jit_solution(8822823792772040538)
XLA Ops:
  1.9 139.0 %shard_map.131 = (f32[2,8,256,128]{3,2,1,0:T(8,128)S(1)}, f32[8,128]{1,0:T(8,128)S(1)}) custom-call(f32[2,8,256,128]{3,2,1,0:T(8,128)} %bitcast.5, bf16[3,8,32,256]{3,2,1,0:T(8,128)(2,1)} %velocity.1, s32[1]{0:T(128)S(6)} %copy.16.species, f32[1,64]{1,0:T(1,128)} %bitcast.6, s32[1]{0:T(128)S(6)} %copy.17.bound, bf16[512,512]{1,0:T(8,128)(2,1)} %constant.25.rest_0_, ...), custom_call_target="tpu_custom_call" | custom-call | tf_op jit(solution)/shard_map/pallas_call | solution.py:569
  140.9 0.5 slice.3
  141.4 1.3 copy.15

commit v5 on v4

--- a/solution.py
+++ b/solution.py
@@ -364,14 +364,15 @@
             def _():
                 back_copy(turn, quad, slot, peer, 3).start()
 
-    def send_rows(turn):
-        @pl.loop(0, quads)
-        def _(quad):
+    def send_rows(turn, after=None):
+        for quad in range(quads):
             for slot in range(len(kept)):
-                start = pl.multiple_of(slot * 2 * rows + quad * 8, 8)
-                block = jnp.swapaxes(flat[:, pl.ds(start, 8), :], 0, 1).reshape(4, 2 * planes, half)
+                start = slot * 2 * rows + quad * 8
+                block = jnp.swapaxes(flat[:, start : start + 8, :], 0, 1).reshape(4, 2 * planes, half)
                 back_sent[quad, slot] = packed(block).astype(BF16)
             start_rows(turn, quad)
+            if after is not None and quad == 0:
+                after()
 
             @pl.when(keeps)
             def _():
@@ -482,14 +483,15 @@
         jnp.where(lane == 1, whole(jnp.sum, grad_part), whole(jnp.max, peak)),
     )[None]
 
-    @pl.loop(1, parts)
-    def _(k):
-        pltpu.make_async_remote_copy(
-            src_ref=stats.at[me], dst_ref=stats.at[me], send_sem=stat_send_sem, recv_sem=stat_sem,
-            device_id={"fft": lax.rem(me + k, parts)}, device_id_type=MESH,
-        ).start()
-
-    send_rows(0)
+    def stats_out():
+        @pl.loop(1, parts)
+        def _(k):
+            pltpu.make_async_remote_copy(
+                src_ref=stats.at[me], dst_ref=stats.at[me], send_sem=stat_send_sem, recv_sem=stat_sem,
+                device_id={"fft": lax.rem(me + k, parts)}, device_id_type=MESH,
+            ).start()
+
+    send_rows(0, stats_out)
     wait_sent(0)
     everyone = stats.at[pl.ds(0, parts - 1)]
     stat_wait = pltpu.make_async_remote_copy(

time: 143 us -> 141 us (0.986)
  Pallas kernels: 139 us -> 137 us
    pallas_call x1, Pallas kernels: 139 us -> 137 us  [body(): pl.pallas_call(functools.partial(kernel, parts, groups, near), out_shape=...]
where the time goes in v5:
time: 141 us; the launch traced here: 140 us
  Pallas kernels  137 us (97%)
  between operations  1.93 us (1%)
  local copies, waits for them, and re-layouts  1.83 us (1%)
    pallas_call x1, Pallas kernels, body(): pl.pallas_call(functools.partial(kernel, parts, groups, near), out_shape=...  137 us

profile of v5, /device:TPU:1, one launch (start us, length us, event | category | flops | bytes accessed | tf_op | source)
XLA Modules:
  0.0 140.5 jit_solution(2530153508448292279)
XLA Ops:
  1.9 136.7 %shard_map.131 = (f32[2,8,256,128]{3,2,1,0:T(8,128)S(1)}, f32[8,128]{1,0:T(8,128)S(1)}) custom-call(f32[2,8,256,128]{3,2,1,0:T(8,128)} %bitcast.5, bf16[3,8,32,256]{3,2,1,0:T(8,128)(2,1)} %velocity.1, s32[1]{0:T(128)S(6)} %copy.16.species, f32[1,64]{1,0:T(1,128)} %bitcast.6, s32[1]{0:T(128)S(6)} %copy.17.bound, bf16[512,512]{1,0:T(8,128)(2,1)} %constant.25.rest_0_, ...), custom_call_target="tpu_custom_call" | custom-call | tf_op jit(solution)/shard_map/pallas_call | solution.py:571
  138.6 0.5 slice.3
  139.1 1.3 copy.15

commit v6 on v5

--- a/solution.py
+++ b/solution.py
@@ -118,8 +118,12 @@
         pltpu.make_async_copy(src, dst, table_sem.at[k])
         for k, (src, dst) in enumerate(zip(far_tables, (z_inv, y_inv, y_inv_turned, y_fwd, z_fwd, x_inv, x_fwd)))
     ]
-    state_copy = pltpu.make_async_copy(state_in, state, state_sem)
-    state_copy.start()
+    state_copies = [
+        pltpu.make_async_copy(state_in.at[:, pl.ds(k * 4, 4)], state.at[:, pl.ds(k * 4, 4)], state_sem.at[k])
+        for k in range(2)
+    ]
+    for copy in state_copies:
+        copy.start()
     table_copies[0].start()
     barrier = pltpu.get_barrier_semaphore()
 
@@ -155,11 +159,12 @@
     def fold(x):
         return jnp.sum(x.reshape(length // 8, 8, half), axis=0)
 
-    state_copy.wait()
-
-    @pl.loop(0, rows)
-    def _(row):
-        put_spectrum(row, state[0, row], state[1, row])
+    for k, copy in enumerate(state_copies):
+        copy.wait()
+
+        @pl.loop(4 * k, 4 * k + 4)
+        def _(row):
+            put_spectrum(row, state[0, row], state[1, row])
 
     table_copies[0].wait()
 
@@ -227,13 +232,14 @@
             return 0
 
         lax.fori_loop(0, parts // batch, one_batch, 0)
-        came[:, pl.ds(me, 1)] = sent[me][:, None]
 
         @pl.loop(1, pairs)
         def _(chunk):
             @pl.loop(1, parts)
             def _(i):
                 came_copy(turn, chunk, peer_in_turn(parts - i)).start()
+
+        came[:, pl.ds(me, 1)] = sent[me][:, None]
 
     def wait_planes(turn, chunk):
         piece = sent.at[pl.ds(0, parts - 1), pl.ds(0, 2)]
@@ -575,7 +581,7 @@
         out_specs=(vmem, vmem),
         scratch_shapes=[
             pltpu.VMEM((2, rows, length, half), F32),
-            DMA,
+            DMA((2,)),
             *(pltpu.VMEM(t.shape, t.dtype) for t in tables),
             DMA((len(tables),)),
             pltpu.VMEM((2 * length, rows * 2 * half), BF16),

time: 141 us -> 141 us (level)
  no operation moved by 1% of the time
where the time goes in v6:
time: 141 us; the launch traced here: 140 us
  Pallas kernels  137 us (97%)
  between operations  1.93 us (1%)
  local copies, waits for them, and re-layouts  1.83 us (1%)
    pallas_call x1, Pallas kernels, body(): pl.pallas_call(functools.partial(kernel, parts, groups, near), out_shape=...  137 us

profile of v6, /device:TPU:1, one launch (start us, length us, event | category | flops | bytes accessed | tf_op | source)
XLA Modules:
  0.0 140.5 jit_solution(10152417307755350905)
XLA Ops:
  1.9 136.7 %shard_map.131 = (f32[2,8,256,128]{3,2,1,0:T(8,128)S(1)}, f32[8,128]{1,0:T(8,128)S(1)}) custom-call(f32[2,8,256,128]{3,2,1,0:T(8,128)} %bitcast.5, bf16[3,8,32,256]{3,2,1,0:T(8,128)(2,1)} %velocity.1, s32[1]{0:T(128)S(6)} %copy.16.species, f32[1,64]{1,0:T(1,128)} %bitcast.6, s32[1]{0:T(128)S(6)} %copy.17.bound, bf16[512,512]{1,0:T(8,128)(2,1)} %constant.25.rest_0_, ...), custom_call_target="tpu_custom_call" | custom-call | tf_op jit(solution)/shard_map/pallas_call | solution.py:577
  138.7 0.5 slice.3
  139.2 1.3 copy.15
